TPU v7x, 256 devices: a whole 4x4x8 slice. The times are simulated.
256 devices in a mesh: dp: 256 (over z, y, x, core).
Axes of the slice: x: 4, y: 4, z: 8, core: 2. Of those that a mesh axis runs over, the one named last changes fastest.
Arguments:
- user_x: float32 [32768, 256], P('dp')
- item_x: float32 [32768, 256], P('dp')
- item_id: int32 [32768], P('dp')
- log_q: float32 [32768], P('dp')
- user_w1: float32 [256, 384], replicated
- user_w2: float32 [384, 384], replicated
- user_w3: float32 [384, 128], replicated
- item_w1: float32 [256, 384], replicated
- item_w2: float32 [384, 384], replicated
- item_w3: float32 [384, 128], replicated
Outputs:
- output 1: float32 [], replicated
- output 2: float32 [256, 384], replicated
- output 3: float32 [384, 384], replicated
- output 4: float32 [384, 128], replicated
- output 5: float32 [256, 384], replicated
- output 6: float32 [384, 384], replicated
- output 7: float32 [384, 128], replicated
All inputs are finite; a program needn't handle non-finite values.
Results may differ from a plain program's by a relative error of at most 0.00200594.
Values are sent between devices in bfloat16 or wider.
A program may use at most 768 MiB of HBM per device.

v0:
```python
import jax
import jax.numpy as jnp
from jax import lax
from jax.sharding import PartitionSpec as P

value_a11 = 0.05
INV_TEMP = 1.0 / value_a11
NORM_EPS = 1e-6
ROW_DIMS = (((0,), (0,)), ((), ()))
COL_DIMS = (((1,), (1,)), ((), ()))


def tower_forward(inputs, w_one, w_two, w_three):
    x_half = inputs.astype(jnp.bfloat16)
    pre_one = jnp.dot(x_half, w_one, preferred_element_type=jnp.float32)
    act_one = jnp.maximum(pre_one, 0.0).astype(jnp.bfloat16)
    pre_two = jnp.dot(act_one, w_two, preferred_element_type=jnp.float32)
    act_two = jnp.maximum(pre_two, 0.0).astype(jnp.bfloat16)
    raw_out = jnp.dot(act_two, w_three, preferred_element_type=jnp.float32)
    inv_norm = lax.rsqrt(jnp.sum(raw_out * raw_out, axis=1, keepdims=True) + NORM_EPS)
    return (x_half, pre_one, act_one, pre_two, act_two, raw_out * inv_norm, inv_norm)


def tower_backward(saved, w_two, w_three, grad_unit):
    x_half, pre_one, act_one, pre_two, act_two, unit_out, inv_norm = saved
    grad_raw = inv_norm * (grad_unit - unit_out * jnp.sum(unit_out * grad_unit, axis=1, keepdims=True))
    grad_raw_h = grad_raw.astype(jnp.bfloat16)
    grad_three = lax.dot_general(act_two, grad_raw_h, ROW_DIMS, preferred_element_type=jnp.float32)
    grad_act_two = lax.dot_general(grad_raw_h, w_three, COL_DIMS, preferred_element_type=jnp.float32)
    grad_pre_two = jnp.where(pre_two > 0.0, grad_act_two, 0.0).astype(jnp.bfloat16)
    grad_two = lax.dot_general(act_one, grad_pre_two, ROW_DIMS, preferred_element_type=jnp.float32)
    grad_act_one = lax.dot_general(grad_pre_two, w_two, COL_DIMS, preferred_element_type=jnp.float32)
    grad_pre_one = jnp.where(pre_one > 0.0, grad_act_one, 0.0).astype(jnp.bfloat16)
    grad_one = lax.dot_general(x_half, grad_pre_one, ROW_DIMS, preferred_element_type=jnp.float32)
    return (grad_one, grad_two, grad_three)


def solution(mesh):
    def device_step(user_x, item_x, item_id, log_q, user_w1, user_w2, user_w3, item_w1, item_w2, item_w3):
        user_ws = (user_w1.astype(jnp.bfloat16), user_w2.astype(jnp.bfloat16), user_w3.astype(jnp.bfloat16))
        item_ws = (item_w1.astype(jnp.bfloat16), item_w2.astype(jnp.bfloat16), item_w3.astype(jnp.bfloat16))
        user_saved = tower_forward(user_x, user_ws[0], user_ws[1], user_ws[2])
        item_saved = tower_forward(item_x, item_ws[0], item_ws[1], item_ws[2])
        user_half = user_saved[5].astype(jnp.bfloat16)
        item_half = item_saved[5].astype(jnp.bfloat16)
        item_all = lax.all_gather(item_half, 'dp', axis=0, tiled=True)
        logq_all = lax.all_gather(log_q, 'dp', axis=0, tiled=True)
        id_all = lax.all_gather(item_id, 'dp', axis=0, tiled=True)
        local_rows = user_x.shape[0]
        batch = item_all.shape[0]
        query_pos = lax.axis_index('dp') * local_rows + jnp.arange(local_rows)
        cand_pos = jnp.arange(batch)
        is_self = query_pos[:, None] == cand_pos[None, :]
        dropped = jnp.logical_and(item_id[:, None] == id_all[None, :], jnp.logical_not(is_self))
        raw = lax.dot_general(user_half, item_all, COL_DIMS, preferred_element_type=jnp.float32) * INV_TEMP - logq_all[None, :]
        scores = jnp.where(dropped, -jnp.inf, raw)
        row_max = jnp.max(scores, axis=1, keepdims=True)
        exp_scores = jnp.exp(scores - row_max)
        row_total = jnp.sum(exp_scores, axis=1, keepdims=True)
        log_norm = row_max[:, 0] + jnp.log(row_total[:, 0])
        pos_score = jnp.sum(user_half.astype(jnp.float32) * item_half.astype(jnp.float32), axis=1) * INV_TEMP - log_q
        softmax_rows = exp_scores / row_total
        grad_scores = (jnp.where(is_self, softmax_rows - 1.0, softmax_rows) / batch).astype(jnp.bfloat16)
        grad_user = jnp.dot(grad_scores, item_all, preferred_element_type=jnp.float32) * INV_TEMP
        item_part = lax.dot_general(grad_scores, user_half, ROW_DIMS, preferred_element_type=jnp.float32) * INV_TEMP
        grad_item = lax.psum_scatter(item_part, 'dp', scatter_dimension=0, tiled=True)
        user_grads = tower_backward(user_saved, user_ws[1], user_ws[2], grad_user)
        item_grads = tower_backward(item_saved, item_ws[1], item_ws[2], grad_item)
        totals = lax.psum((jnp.sum(log_norm - pos_score),) + user_grads + item_grads, 'dp')
        return (totals[0] / batch,) + tuple(totals[1:])

    batch_spec = P('dp', None)
    vec_spec = P('dp')
    whole = P()
    return jax.shard_map(device_step, mesh=mesh,
                         in_specs=(batch_spec, batch_spec, vec_spec, vec_spec, whole, whole, whole, whole, whole, whole),
                         out_specs=(whole, whole, whole, whole, whole, whole, whole), check_vma=False)
```

profile of v0, /device:TPU:1, one launch (start us, length us, event | category | flops | bytes accessed | tf_op | source)
XLA Modules:
  0.0 1802.5 jit_solution(14923689951901798100)
XLA Ops:
  7.2 0.0 all-gather.4.cloned.1.call-start
  7.2 1.3 fusion.13
  8.5 1.3 fusion.23
  9.7 1.2 multiply_reduce_fusion.4
  10.9 1.3 fusion.11
  12.2 1.3 fusion.19
  13.5 1.2 multiply_reduce_fusion.3
  14.6 0.6 multiply_reduce_fusion.2
  15.3 0.0 all-gather.4.cloned.1.call-update
  15.3 0.0 reduce-scatter.2.cloned.1.call-start
  15.4 79.0 %all-gather.1 = f32[256,1,128]{2,1,0:T(1,128)S(1)} all-gather(f32[1,1,128]{2,1,0:T(1,128)} %bitcast.24), channel_id=1, replica_groups=mesh['dp'=256] {'dp'}, dimensions={0}, use_global_device_ids=true | all-gather | bytes 131584 | tf_op jit(solution)/shard_map/all_gather | solution.py:47
  94.3 71.6 %all-gather = s32[256,1,128]{2,1,0:T(1,128)S(1)} all-gather(s32[1,1,128]{2,1,0:T(1,128)} %bitcast.25), channel_id=1, replica_groups=mesh['dp'=256] {'dp'}, dimensions={0}, use_global_device_ids=true | all-gather | bytes 131584 | tf_op jit(solution)/shard_map/all_gather | solution.py:48
  165.9 0.0 all-gather.4.cloned.1.call-done
  165.9 13.4 fusion.51
  179.3 8.2 fusion.6
  187.6 8.4 fusion.3
  196.0 0.0 copy-start
  196.0 3.2 copy-done
  199.2 8.1 convolution_multiply_fusion
  207.3 0.0 reduce-scatter.2.cloned.1.call-update
  207.3 0.0 copy-start.3
  207.3 0.0 copy-start.1
  207.3 0.0 copy-start.5
  207.3 0.0 copy-start.4
  207.3 0.0 copy-start.2
  207.3 0.0 copy-start.6
  207.3 0.0 copy-start.7
  207.4 0.2 all-reduce.3.cloned.1.call-start
  207.6 8.3 multiply_reduce_fusion.1
  215.9 0.9 fusion.34
  216.8 0.0 copy-done.3
  216.8 0.2 fusion.7
  217.0 1.1 fusion.33
  218.1 0.0 copy-done.1
  218.1 0.0 copy-done.5
  218.1 1.2 convolution_bitcast_fusion.1
  219.4 1287.3 %reduce-scatter.2.cloned.1.call-done = f32[128,128]{0,1:T(8,128)} async-done(((f32[32768,128]{0,1:T(8,128)}), f32[128,128]{0,1:T(8,128)}) %reduce-scatter.2.cloned.1.call-update) | async-done | bytes 65552 | tf_op jit(solution)/shard_map/reduce_scatter | solution.py:66
  1506.7 0.9 multiply_reduce_fusion
  1507.6 0.9 multiply_convert_fusion
  1508.4 0.0 copy-done.4
  1508.4 0.2 fusion.9
  1508.7 0.9 fusion.36
  1509.6 0.0 copy-done.2
  1509.6 0.0 copy-done.6
  1509.6 1.2 convolution_bitcast_fusion
  1510.8 1.1 fusion.35
  1511.9 0.0 all-reduce.3.cloned.1.call-update
  1511.9 0.0 copy-done.7
  1511.9 0.6 subtract_reduce_fusion
  1512.5 80.2 %psum.49 = f32[]{:T(128)} all-reduce(f32[]{:T(128)} %subtract_reduce_fusion), channel_id=1, replica_groups=mesh['dp'=256] {'dp'}, use_global_device_ids=true, to_apply=%region_6.7 | all-reduce | flops 1 | bytes 8 | tf_op jit(solution)/shard_map/psum | solution.py:69
  1593.4 190.6 %all-reduce.3.cloned.1.call-done = (f32[256,384]{0,1:T(8,128)}, f32[384,384]{1,0:T(8,128)}, f32[384,128]{1,0:T(8,128)}, f32[256,384]{0,1:T(8,128)}, f32[384,384]{1,0:T(8,128)}, /*index=5*/f32[384,128]{1,0:T(8,128)}) async-done(((f32[256,384]{0,1:T(8,128)}, f32[384,384]{1,0:T(8,128)}, f32[384,128]{1,0:T(8,128)}, f32[256,384]{0,1:T(8,128)}, f32[384,384]{1,0:T(8,128)}, /*index=5*/f32[384,128]{1,0:T(8,128)}), ...) | async-done | bytes 2359312 | tf_op jit(solution)/shard_map/psum | solution.py:69
  1784.0 1.9 copy.21
  1785.9 1.9 copy.22
  1787.8 1.9 copy.30
  1789.7 1.6 copy.31
  1791.3 1.9 copy.32
  1793.2 1.6 copy.33
  (3 shorter events, 0.0 us)
Async XLA Ops:
  7.2 158.7 %all-gather.4.cloned.1.call-start = ((), (), s32[]{:S(2)}) async-start(), calls=%async_computation.1 | async-start | bytes 8421376 | tf_op jit(solution)/shard_map/all_gather | solution.py:46
  15.3 1491.4 %reduce-scatter.2.cloned.1.call-start = ((), (), s32[]{:S(2)}) async-start(), calls=%async_computation.2 | async-start | bytes 16842752 | tf_op jit(solution)/shard_map/reduce_scatter | solution.py:66
  196.0 3.2 copy-start
  207.3 9.5 copy-start.3
  207.3 10.8 copy-start.1
  207.3 10.8 copy-start.5
  207.3 1301.1 %copy-start.4 = (f32[384,128]{1,0:T(8,128)S(1)}, f32[384,128]{1,0:T(8,128)}, u32[]{:S(2)}) copy-start(f32[384,128]{1,0:T(8,128)} %param.19) | copy-start | bytes 589828
  207.3 1302.2 %copy-start.2 = (f32[384,384]{1,0:T(8,128)S(1)}, f32[384,384]{1,0:T(8,128)}, u32[]{:S(2)}) copy-start(f32[384,384]{1,0:T(8,128)} %param.18) | copy-start | bytes 1769476
  207.3 1302.2 %copy-start.6 = (f32[128,256]{1,0:T(8,128)S(1)}, f32[128,256]{1,0:T(8,128)}, u32[]{:S(2)}) copy-start(f32[128,256]{1,0:T(8,128)} %param.11) | copy-start | bytes 393220
  207.3 1304.6 %copy-start.7 = (f32[128]{0:T(128)S(1)}, f32[128]{0:T(128)}, u32[]{:S(2)}) copy-start(f32[128]{0:T(128)} %param.13) | copy-start | bytes 1540
  207.4 1576.6 %all-reduce.3.cloned.1.call-start = ((), (), s32[]{:S(2)}) async-start(), calls=%async_computation.3 | async-start | bytes 4718592 | tf_op jit(solution)/shard_map/psum | solution.py:69
Sparse Core Ops, SparseCore 0:
  15.4 122.2 all-gather.3
  207.4 1299.2 reduce-scatter.1
  1513.7 270.1 all-reduce.2
where the time goes:
time: 1800 us
  waiting for transfers between devices  1480 us (82%)
  blocking collectives  231 us (13%)
  matrix products  44 us (2%)
  other arithmetic  19.6 us (1%)
    reduce_scatter x1, waiting for transfers between devices, device_step(): lax.psum_scatter(item_part, 'dp', scatter_dimension=0, tiled=True)  1290 us
    psum x1, waiting for transfers between devices, device_step(): lax.psum((jnp.sum(log_norm - pos_score),) + user_grads + item_grads, 'dp')  191 us
    psum x1, blocking collectives, device_step(): lax.psum((jnp.sum(log_norm - pos_score),) + user_grads + item_grads, 'dp')  80.2 us
    all_gather x1, blocking collectives, device_step(): logq_all = lax.all_gather(log_q, 'dp', axis=0, tiled=True)  79 us
    all_gather x1, blocking collectives, device_step(): id_all = lax.all_gather(item_id, 'dp', axis=0, tiled=True)  71.6 us
  transfers between devices with their start and end apart: 3, of which 2 were waited for; matrix products, arithmetic and copies ran while one was open for 1% of the time, Pallas kernels for 0%

commit v1 on v0

v1 whole, which is shorter than its diff:
```python
import functools
import math

import jax
import jax.numpy as jnp
from jax import lax
from jax.experimental import pallas as pl
from jax.experimental.pallas import tpu as pltpu
from jax.sharding import PartitionSpec as P

F32, BF16, I32 = jnp.float32, jnp.bfloat16, jnp.int32
MESH = pl.DeviceIdType.MESH

GRID = {256: (8, 4, 4)}
UNITS_PER_Z = None

L, SUB = 128, 8
PAIR = range(2)
USER, ITEM = PAIR
W_IN, W_A, W_B = 256, 384, 384
DUO = 2 * L
MAX_GROUPS = 32
TEMP = 0.05
INV_TEMP = 1.0 / TEMP
EXP_SCALE = INV_TEMP * math.log2(math.e)
NORM_EPS = 1e-6
LOW = -3.0e38
ROWS_1, ROWS_2, ROWS_3 = W_IN * W_A // L, W_A * W_B // L, W_B
AT_2, AT_3 = ROWS_1, ROWS_1 + ROWS_2
GRAD_ROWS = AT_3 + ROWS_3
HALF_ROWS = GRAD_ROWS // 2
COLS = W_A // L
X_AT, H1_AT, H2_AT, ACT_ROWS = 0, W_IN, W_IN + W_A, W_IN + W_A + W_B
VMEM_BYTES, LAYOUT_BYTES = 56 << 20, 1 << 20
LAG_V, LAG_DV = 4, 5
NN = (((1,), (0,)), ((), ()))
NT = (((1,), (1,)), ((), ()))


def _dot(a, b, dims=NN):
    return lax.dot_general(a, b, dims, preferred_element_type=F32)


def _near(k):
    return k + k // 2 - 2 * (k // 3)


def _lanes(j, n=1):
    return slice(j * L, (j + n) * L)


def _at(start, size):
    return pl.ds(pl.multiple_of(start, SUB), size)


def _peers(n):
    return range(1, n)


def _iota(shape, dim):
    return lax.broadcasted_iota(I32, shape, dim)


class _Marks:
    def __init__(self):
        self.scope = None

    def __call__(self, name=None):
        if self.scope is not None:
            self.scope.__exit__(None, None, None)
        self.scope = jax.named_scope(name) if name else None
        if name:
            self.scope.__enter__()


class _Plan:
    def __init__(self, n):
        nz, ny, nx = self.nz, self.ny, self.nx = GRID[n]
        self.plane = nx * ny
        self.batch = n * L
        self.queries = nz * L
        self.c2 = HALF_ROWS // self.plane
        self.n1, self.n2 = (nx, ny), (ny, nx)
        self.c1 = tuple(HALF_ROWS // m for m in self.n1)
        self.w = (UNITS_PER_Z or self.c2 // SUB // nz) * SUB
        self.rest = self.c2 - nz * self.w
        self.tail = 2 * self.rest + SUB
        self.offsets = [(_near(k // nx), _near(k % nx)) for k in range(self.plane)]
        self.zorder = sorted(range(nz), key=lambda d: -min(d, nz - d))
        self.own = self.zorder.index(0)

    def slot(self, dy, dx):
        return self.offsets.index((dy % self.ny, dx % self.nx))

    def tile(self, dz):
        return self.zorder.index(dz % self.nz)


def _scratch(p):
    npl, nz, nq = p.plane, p.nz, p.queries
    vm, dma = pltpu.VMEM, pltpu.SemaphoreType.DMA
    groups, most = 2 * npl, max(p.n1)
    nrx = max(groups, 2 * nz)
    a1 = p.c1[0] + SUB
    return dict(
        xs=vm((2, L, W_IN), F32),
        wf1=vm((2, W_IN, W_A), F32),
        wf2=vm((2, W_A, W_B), F32),
        wf3=vm((2, W_B, L), F32),
        w2=vm((2, W_A, W_B), BF16),
        w3=vm((2, W_B, L), BF16),
        acts=vm((2, ACT_ROWS, DUO), BF16),
        hid=vm((2, DUO, W_A + W_B), BF16),
        unit=vm((2, DUO, DUO), F32),
        idb=vm((groups, 1, L), I32),
        lqb=vm((groups, 1, L), F32),
        idq=vm((nz, 1, L), I32),
        idk=vm((MAX_GROUPS, L), I32),
        lqk=vm((MAX_GROUPS, L), F32),
        idc=vm((npl, DUO, L), I32),
        vaug=vm((npl, DUO, DUO), BF16),
        vt=vm((npl, L, DUO), BF16),
        uall=vm((nq, L), BF16),
        ut=vm((DUO, nq), BF16),
        tb=vm((npl, DUO, nq), F32),
        ls=vm((SUB, nq), F32),
        dg=vm((1, L), F32),
        stat=vm((nz, 2, nq), F32),
        fac=vm((2, nq), F32),
        gt=vm((npl, DUO, nq), BF16),
        dvp=vm((npl, DUO, L), F32),
        dvs=vm((npl, L, L), F32),
        dvo=vm((npl, L, L), F32),
        dut=vm((nz, L, L), F32),
        rx=vm((nrx, L, L), F32),
        de=vm((DUO, L), F32),
        ga=vm((p.n1[0] * a1, L), F32),
        gb=vm((HALF_ROWS, L), F32),
        r1a=vm((most, a1, L), F32),
        r1b=vm((most, p.c1[1], L), F32),
        s1a=vm((a1, L), F32),
        s1b=vm((p.c1[1], L), F32),
        r2a=vm((most, p.c2 + SUB, L), F32),
        r2b=vm((most, p.c2, L), F32),
        s2=vm((nz * 2 * p.w + p.tail, L), F32),
        r3=vm((nz, 2 * p.w + p.tail, L), F32),
        f2=vm((nz * 2 * p.w, L), F32),
        lossb=vm((2, SUB, L), F32),
        ld=dma((3 + 2 * 4,)),
        sm_s=dma((3,)),
        sm_r=dma((3,)),
        v_s=dma((npl,)),
        v_r=dma((npl,)),
        fw_s=dma((npl,)),
        fw_r=dma((npl,)),
        u_s=dma((nz,)),
        u_r=dma((nz,)),
        ac_s=dma((3,)),
        ac_r=dma((3,)),
        st_s=dma((nz,)),
        st_r=dma((nz,)),
        dv_s=dma((npl,)),
        dv_r=dma((npl,)),
        do_s=dma((npl,)),
        du_s=dma((nz,)),
        rx_r=dma((nrx,)),
        p1_s=dma((2, most)),
        p1_r=dma((2, most)),
        p2_s=dma((3, most)),
        p2_r=dma((3, most)),
        p3_s=dma((2, nz)),
        p3_r=dma((2, nz)),
        p4_s=dma((nz,)),
        p4_r=dma((nz,)),
        p5_s=dma((2, most)),
        p5_r=dma((2, most)),
        p6_s=dma((2, most)),
        p6_r=dma((2, most)),
        sb_s=dma((2, most)),
        sb_r=dma((2, most)),
        ls_s=dma(()),
        ls_r=dma(()),
    )


def _kernel(p, names, ux, ix, ids, lq, uw1, uw2, uw3, iw1, iw2, iw3, fin, loss, *refs):
    s = dict(zip(names, refs, strict=True))
    nz, ny, nx, npl, nq = p.nz, p.ny, p.nx, p.plane, p.queries
    half = nz // 2
    mark = _Marks()
    me = lax.axis_index("dp")
    c = lax.rem(me, 2)
    chip = lax.div(me, 2)
    x = lax.rem(chip, nx)
    y = lax.rem(lax.div(chip, nx), ny)
    z = lax.div(chip, nx * ny)
    sibling = me + 1 - 2 * c

    def dev(dz, dy, dx, core):
        zz, yy, xx = lax.rem(z + dz, nz), lax.rem(y + dy, ny), lax.rem(x + dx, nx)
        return ((zz * ny + yy) * nx + xx) * 2 + core

    def rcopy(src, dst, send, recv, to):
        return pltpu.make_async_remote_copy(
            src_ref=src, dst_ref=dst, send_sem=send, recv_sem=recv, device_id=(to,), device_id_type=MESH
        )

    sends = []

    def send(src, dst, ssem, rsem, to):
        cp = rcopy(src, dst, ssem, rsem, to)
        cp.start()
        sends.append(cp)

    def arrived(dst, rsem):
        rcopy(dst, dst, rsem, rsem, me).wait_recv()

    lane = pl.ds(pl.multiple_of(c * L, L), L)
    other = pl.ds(pl.multiple_of((1 - c) * L, L), L)

    mark("start")
    xs, idb, lqb, idq, ld = s["xs"], s["idb"], s["lqb"], s["idq"], s["ld"]
    own = p.own
    small = [(ids, idb.at[c]), (lq, lqb.at[c]), (ids, idq.at[own])]
    small = [pltpu.make_async_copy(a, b, ld.at[i]) for i, (a, b) in enumerate(small)]
    loads = {}
    n_ld = len(small)
    for t, given in ((ITEM, (ix, iw1, iw2, iw3)), (USER, (ux, uw1, uw2, uw3))):
        loads[t] = []
        for src, dst in zip(given, (xs, s["wf1"], s["wf2"], s["wf3"]), strict=True):
            loads[t].append(pltpu.make_async_copy(src, dst.at[t], ld.at[n_ld]))
            n_ld += 1
    for cp in small + loads[ITEM] + loads[USER]:
        cp.start()

    barrier = pltpu.get_barrier_semaphore()
    others = [dev(0, dy, dx, core) for core in PAIR for dy, dx in p.offsets[1:]]
    others += [dev(dz, 0, 0, core) for core in PAIR for dz in _peers(nz)]
    others.append(sibling)
    for to in others:
        pl.semaphore_signal(barrier, inc=1, device_id=(to,), device_id_type=MESH)

    acts, hid, unit = s["acts"], s["hid"], s["unit"]

    def tower(t):
        place = jnp.where(c == t, 0, 1)
        for cp in loads[t]:
            cp.wait()
        w1, w2, w3 = s["wf1"][t].astype(BF16), s["wf2"][t].astype(BF16), s["wf3"][t].astype(BF16)
        s["w2"][t], s["w3"][t] = w2, w3
        xh = xs[t].astype(BF16)
        h1 = jnp.maximum(_dot(xh, w1), 0.0).astype(BF16)
        h2 = jnp.maximum(_dot(h1, w2), 0.0).astype(BF16)
        raw = _dot(h2, w3)
        inv = lax.rsqrt(jnp.sum(raw * raw, axis=1, keepdims=True) + NORM_EPS)
        e = raw * inv
        acts[place, X_AT:H1_AT, lane] = xh.T
        acts[place, H1_AT:H2_AT, lane] = h1.T
        acts[place, H2_AT:ACT_ROWS, lane] = h2.T
        hid[place, lane, :W_A] = h1
        hid[place, lane, W_A:] = h2
        unit[place, lane, :L] = e
        unit[place, lane, L:] = jnp.broadcast_to(inv, (L, L))
        return e.astype(BF16)

    mark("towers")
    vaug, uall = s["vaug"], s["uall"]
    vaug[0, lane, :L] = tower(ITEM)
    uall[_lanes(own), :] = tower(USER)
    for cp in small:
        cp.wait()
    mark("barrier_wait")
    pl.semaphore_wait(barrier, len(others))

    mark("send_uv")
    sm_s, sm_r = s["sm_s"], s["sm_r"]

    def send_small(k, to):
        rcopy(idb.at[c], idb.at[2 * k + c], sm_s.at[0], sm_r.at[0], to).start()
        rcopy(lqb.at[c], lqb.at[2 * k + c], sm_s.at[1], sm_r.at[1], to).start()

    send_small(0, sibling)
    for dy, dx in p.offsets[1:]:
        for core in PAIR:
            send_small(p.slot(-dy, -dx), dev(0, dy, dx, core))
    n_small = 2 * npl - 1
    for dz in _peers(nz):
        rcopy(idq.at[own], idq.at[p.tile(-dz)], sm_s.at[2], sm_r.at[2], dev(dz, 0, 0, c)).start()

    def vpart(k, rows):
        return vaug.at[k, rows, pl.ds(0, L)]

    def upart(j):
        return uall.at[_lanes(j)]

    send(vpart(0, lane), vpart(0, lane), s["fw_s"].at[0], s["fw_r"].at[0], sibling)
    for i in range(1, max(npl, nz)):
        if i < nz:
            dz = p.zorder[-1 - i]
            send(upart(own), upart(p.tile(-dz)), s["u_s"].at[dz], s["u_r"].at[p.tile(-dz)], dev(dz, 0, 0, c))
        if i < npl:
            dy, dx = p.offsets[i]
            k = p.slot(-dy, -dx)
            send(vpart(0, lane), vpart(k, lane), s["v_s"].at[i], s["v_r"].at[k], dev(0, dy, dx, c))
    for i, part in enumerate(((acts, slice(None), lane), (hid, lane, slice(None)), (unit, lane, slice(None)))):
        ref, rows, cols = part
        send(ref.at[1, rows, cols], ref.at[0, rows, cols], s["ac_s"].at[i], s["ac_r"].at[i], sibling)

    mark("small_wait")
    idk, lqk, idc, ut = s["idk"], s["lqk"], s["idc"], s["ut"]
    idk[...] = jnp.full(idk.shape, -1, I32)
    lqk[...] = jnp.full(lqk.shape, -LOW, F32)
    ut[L:, :] = jnp.where(_iota((L, nq), 0) < 3 * MAX_GROUPS, -1.0, 0.0).astype(BF16)
    for i, (ref, n) in enumerate(((idb, n_small), (lqb, n_small), (idq, nz - 1))):
        if n:
            pltpu.make_async_copy(ref.at[pl.ds(0, n)], ref.at[pl.ds(0, n)], sm_r.at[i]).wait()
    mark("turn")
    for g in range(2 * npl):
        row = idb[g]
        idk[g : g + 1, :] = row
        lqk[g : g + 1, :] = lqb[g] * TEMP
        idc[g // 2, _lanes(g % 2), :] = jnp.broadcast_to(row, (L, L)).T

    def parts(q):
        hi = q.astype(BF16).astype(F32)
        mid = (q - hi).astype(BF16).astype(F32)
        return hi, mid, (q - hi - mid).astype(BF16).astype(F32)

    q_all, id_all = lqk[...], idk[...]
    split = parts(jnp.where(id_all < 0, 0.0, q_all))
    turned = jnp.concatenate([*split, jnp.zeros((MAX_GROUPS, L), F32)], axis=0).T.astype(BF16)
    col = _iota((L, L), 1)
    ones = jnp.where(col < 3 * MAX_GROUPS + 3, 1.0, 0.0)
    for g in range(2 * npl):
        keep = jnp.where(col < 3 * MAX_GROUPS, jnp.where(lax.rem(col, MAX_GROUPS) == g, turned.astype(F32), 0.0), ones)
        vaug[g // 2, _lanes(g % 2), L:] = keep.astype(BF16)

    def most(a):
        return jnp.max(jnp.max(a, axis=0, keepdims=True), axis=1, keepdims=True)

    top1 = most(-q_all)
    at_top = -q_all == top1
    id_hi, id_lo = (id_all // (1 << 16)).astype(F32), (id_all % (1 << 16)).astype(F32)
    top_hi = most(jnp.where(at_top, id_hi, -1.0))
    top_lo = most(jnp.where(jnp.logical_and(at_top, id_hi == top_hi), id_lo, -1.0))
    same_top = jnp.logical_and(id_hi == top_hi, id_lo == top_lo)
    top2 = most(jnp.where(same_top, LOW, -q_all))
    top2 = jnp.where(top2 <= LOW, top1, top2)
    id_top = top_hi.astype(I32) * (1 << 16) + top_lo.astype(I32)
    stat = s["stat"]
    bounds = []
    for j in range(nz):
        rest = top2
        if j == own:
            rest = jnp.maximum(top2, -lqb[c] * TEMP)
        bounds.append(jnp.where(idq[j] == id_top, rest, jnp.broadcast_to(top1, (1, L))))
    bound = jnp.concatenate(bounds, axis=1)
    stat[0, :1, :] = bound
    at = L + 3 * MAX_GROUPS
    ut[at : at + 16, :] = jnp.concatenate([-a for a in parts(bound)] + [jnp.zeros((16 - 3, nq), F32)], axis=0).astype(BF16)

    mark("u_wait")
    for j in reversed(range(nz)):
        if j != own:
            arrived(upart(j), s["u_r"].at[j])
        ut[:L, _lanes(j)] = uall[_lanes(j), :].T

    mark("pass1")
    tb, ls, vt, dg = s["tb"], s["ls"], s["vt"], s["dg"]
    ls[...] = jnp.zeros(ls.shape, F32)
    diag = _iota((DUO, L), 0) == _iota((DUO, L), 1) + c * L

    def pass1(k, mine):
        for j in range(half):
            wide = _dot(vaug[k], ut[:, _lanes(2 * j, 2)])
            for i in PAIR:
                r = 2 * j + i
                t = wide[:, _lanes(i)]
                drop = idc[k] == idq[r]
                if mine and r == own:
                    drop = jnp.logical_and(drop, jnp.logical_not(diag))
                    dg[...] = jnp.sum(jnp.where(diag, t, 0.0), axis=0, keepdims=True)
                e = jnp.where(drop, 0.0, jnp.exp2(t * EXP_SCALE))
                tb[k, :, _lanes(r)] = e
                ls[:, _lanes(r)] += jnp.sum(e.reshape(DUO // SUB, SUB, L), axis=0)

    def forward(k):
        arrived(vpart(k, lane), s["v_r"].at[k])
        rcopy(vpart(k, lane), vpart(k, lane), s["fw_s"].at[k], s["fw_r"].at[k], sibling).start()

    def step1(k, _):
        @pl.when(k + LAG_V < npl)
        def _():
            forward(k + LAG_V)

        arrived(vpart(k, other), s["fw_r"].at[k])
        pass1(k, False)
        return 0

    for k in range(1, min(LAG_V, npl - 1) + 1):
        forward(k)
    arrived(vpart(0, other), s["fw_r"].at[0])
    pass1(0, True)
    mark("pass1_loop")
    lax.fori_loop(1, npl, step1, 0)

    mark("stat_send")
    stat[0, 1:, :] = jnp.sum(ls[...], axis=0, keepdims=True)
    for dz in _peers(nz):
        send(stat.at[0], stat.at[nz - dz], s["st_s"].at[dz], s["st_r"].at[nz - dz], dev(dz, 0, 0, c))

    def flip(k, _):
        vt[k] = vaug[k, :, :L].T
        return 0

    lax.fori_loop(0, npl, flip, 0)
    mark("stat_wait")
    for dz in _peers(nz):
        arrived(stat.at[dz], s["st_r"].at[dz])

    def theirs(row, dz):
        a = stat[dz, row : row + 1, :]
        return a if dz == 0 else jnp.concatenate([a[:, _lanes(p.tile(d - dz))] for d in p.zorder], axis=1)

    sums = [theirs(1, dz) for dz in range(nz)]
    tops = [jnp.where(a > 0.0, theirs(0, dz), LOW) for dz, a in enumerate(sums)]
    top = functools.reduce(jnp.maximum, tops)
    total = sum(a * jnp.exp2((b - top) * EXP_SCALE) for a, b in zip(sums, tops, strict=True))
    mine = _lanes(own)
    loss_part = (top[:, mine] - bound[:, mine] - dg[...]) * INV_TEMP + jnp.log(total[:, mine])
    loss_tile = jnp.where(_iota((SUB, L), 0) == 0, loss_part, 0.0)
    fac = s["fac"]
    inv_batch = 1.0 / p.batch
    fac[:1, :] = jnp.exp2((tops[0] - top) * EXP_SCALE) * (1.0 / total)
    fac[1:, :] = fac[:1, :] * inv_batch

    gt, dut, dvp, dvs, dvo, rx = s["gt"], s["dut"], s["dvp"], s["dvs"], s["dvo"], s["rx"]
    plane = y * nx + x

    def grads(k, tiles, mine):
        for r in tiles:
            if mine and r == own:
                g = (tb[k, :, _lanes(r)] * fac[:1, _lanes(r)] - jnp.where(diag, 1.0, 0.0)) * inv_batch
            else:
                g = tb[k, :, _lanes(r)] * fac[1:, _lanes(r)]
            gt[k, :, _lanes(r)] = g.astype(BF16)
        first = tiles[0]
        for j in range(len(tiles) // 2):
            part = _dot(vt[k], gt[k, :, _lanes(first + 2 * j, 2)])
            for i in PAIR:
                r = first + 2 * j + i
                piece = part[:, _lanes(i)]
                dut[r] = piece if mine else dut[r] + piece

    def send_du(tiles):
        for j in tiles:
            dz = p.zorder[j]
            if dz:
                send(dut.at[j], rx.at[2 * z + c], s["du_s"].at[dz], s["rx_r"].at[2 * z + c], dev(dz, 0, 0, 0))

    def chip_sum(k):
        arrived(dvs.at[k], s["dv_r"].at[k])
        return dvp[k, lane, :] + dvs[k]

    def finish(k):
        dvo[k] = chip_sum(k)
        to = dev(0, _near(lax.div(k, nx)), _near(lax.rem(k, nx)), 1)
        rcopy(dvo.at[k], rx.at[2 * plane + c], s["do_s"].at[k], s["rx_r"].at[2 * plane + c], to).start()

    far, close = range(half), range(half, nz)
    mark("pass2a")
    grads(0, far, True)

    def step2a(k, _):
        grads(k, far, False)
        return 0

    lax.fori_loop(1, npl, step2a, 0)
    send_du(far)

    mark("pass2b")

    def item_part(k):
        dvp[k] = _dot(gt[k], uall[...])
        rcopy(dvp.at[k, other], dvs.at[k], s["dv_s"].at[k], s["dv_r"].at[k], sibling).start()

    grads(0, close, True)

    def step2b(i, _):
        k = npl - 1 - i
        grads(k, close, False)
        item_part(k)

        @pl.when(i >= LAG_DV)
        def _():
            finish(k + LAG_DV)

        return 0

    lax.fori_loop(0, npl - 1, step2b, 0)
    mark("rs_send")
    send_du(close)
    item_part(0)
    for k in reversed(range(1, min(LAG_DV, npl - 1) + 1)):
        finish(k)
    dvo[0] = chip_sum(0)

    mark("rs_wait")
    de = s["de"]

    def gather(h, acc, order, turn):
        for j in order:
            arrived(rx.at[j], s["rx_r"].at[j])
            acc = rx[j] if acc is None else acc + rx[j]
        de[_lanes(h), :] = (acc.T if turn else acc) * INV_TEMP

    z_from = [lax.rem(z + d, nz) for d in p.zorder if d]
    plane_from = [
        lax.rem(y + ny - dy, ny) * nx + lax.rem(x + nx - dx, nx) for dy, dx in reversed(p.offsets[1:])
    ]

    @pl.when(c == USER)
    def _():
        cp = rcopy(dvo.at[0], rx.at[2 * plane], s["do_s"].at[0], s["rx_r"].at[2 * plane], sibling)
        cp.start()
        gather(0, dut[own], [2 * a for a in z_from], True)
        gather(1, None, [2 * a + 1 for a in [*z_from, z]], True)
        cp.wait_send()

    @pl.when(c == ITEM)
    def _():
        cp = rcopy(dut.at[own], rx.at[2 * z + 1], s["du_s"].at[0], s["rx_r"].at[2 * z + 1], sibling)
        cp.start()
        gather(1, dvo[0], [2 * a + 1 for a in plane_from], False)
        gather(0, None, [2 * a for a in [*plane_from, plane]], False)
        cp.wait_send()

    mark("backward")
    arrived(acts.at[0, :, other], s["ac_r"].at[0])
    arrived(hid.at[0, other, :], s["ac_r"].at[1])
    arrived(unit.at[0, other, :], s["ac_r"].at[2])
    ga, gb = s["ga"], s["gb"]
    c1a, c1b = p.c1
    stride1 = (c1a + SUB, c1b)

    def put(start, val):
        n, done = val.shape[0], 0
        while done < n:
            row = start + done
            color = row // HALF_ROWS
            row -= color * HALF_ROWS
            size = p.c1[color]
            chunk, off = row // size, row % size
            take = min(n - done, size - off)
            to = chunk * stride1[color] + off
            (ga, gb)[color][to : to + take, :] = val[done : done + take]
            done += take

    for i in range(nx):
        ga[(i + 1) * stride1[0] - SUB : (i + 1) * stride1[0], :] = loss_tile
    de_all = de[...]
    e, inv = unit[0, :, :L], unit[0, :, L:]
    dz_h = (inv * (de_all - e * jnp.sum(e * de_all, axis=1, keepdims=True))).astype(BF16)
    put(AT_3, _dot(acts[0, H2_AT:ACT_ROWS, :], dz_h))
    da2 = jnp.where(hid[0, :, W_A:] > 0, _dot(dz_h, s["w3"][c], NT), 0.0).astype(BF16)
    dw2 = _dot(acts[0, H1_AT:H2_AT, :], da2)
    for j in range(COLS):
        put(AT_2 + W_A * j, dw2[:, _lanes(j)])
    da1 = jnp.where(hid[0, :, :W_A] > 0, _dot(da2, s["w2"][c], NT), 0.0).astype(BF16)
    dw1 = _dot(acts[0, X_AT:H1_AT, :], da1)
    for j in range(COLS):
        put(W_IN * j, dw1[:, _lanes(j)])

    mark("ar1_send")
    q1, q2 = (x, y), (y, x)
    g, r1, s1, r2 = (ga, gb), (s["r1a"], s["r1b"]), (s["s1a"], s["s1b"]), (s["r2a"], s["r2b"])
    c2, w, rest, tail = p.c2, p.w, p.rest, p.tail

    def along(axis_x, d):
        return dev(0, 0, d, c) if axis_x else dev(0, d, 0, c)

    def along1(color, d):
        return along(color == 0, d)

    def along2(color, d):
        return along(color == 1, d)

    for d in _peers(max(nx, ny)):
        for color in PAIR:
            n1, st = p.n1[color], stride1[color]
            if d < n1:
                at = _at(lax.rem(q1[color] + d, n1) * st, st)
                send(g[color].at[at], r1[color].at[d], s["p1_s"].at[color, d], s["p1_r"].at[color, d], along1(color, d))
    mark("ar1_wait")
    loss_rows = slice(c1a, c1a + SUB)
    loss_in = slice(c2, c2 + SUB)
    for color in PAIR:
        st = stride1[color]
        acc = g[color][_at(q1[color] * st, st), :]
        for d in _peers(p.n1[color]):
            arrived(r1[color].at[d], s["p1_r"].at[color, d])
            acc = acc + r1[color][d]
        s1[color][...] = acc
        for d in _peers(p.n2[color]):
            at, to = _at(lax.rem(q2[color] + d, p.n2[color]) * c2, c2), along2(color, d)
            send(s1[color].at[at], r2[color].at[d, :c2], s["p2_s"].at[color, d], s["p2_r"].at[color, d], to)
            if color == 0:
                send(s1[0].at[loss_rows], r2[0].at[d, loss_in], s["p2_s"].at[2, d], s["p2_r"].at[2, d], to)
    mark("ar2_wait")
    s2, r3, f2, lossb = s["s2"], s["r3"], s["f2"], s["lossb"]
    base = nz * 2 * w
    for color in PAIR:
        acc = s1[color][_at(q2[color] * c2, c2), :]
        for d in _peers(p.n2[color]):
            arrived(r2[color].at[d, :c2], s["p2_r"].at[color, d])
            acc = acc + r2[color][d, :c2, :]
        for i in range(nz):
            at = (2 * i + color) * w
            s2[at : at + w, :] = acc[i * w : (i + 1) * w]
        if rest:
            s2[base + color * rest : base + (color + 1) * rest, :] = acc[nz * w :]
    acc = s1[0][loss_rows, :]
    for d in _peers(p.n2[0]):
        arrived(r2[0].at[d, loss_in], s["p2_r"].at[2, d])
        acc = acc + r2[0][d, loss_in, :]
    s2[base + 2 * rest :, :] = acc
    own_units, shared = slice(0, 2 * w), slice(2 * w, 2 * w + tail)
    for dz in _peers(nz):
        at, to = _at(lax.rem(z + dz, nz) * 2 * w, 2 * w), dev(dz, 0, 0, c)
        send(s2.at[at], r3.at[dz, own_units], s["p3_s"].at[0, dz], s["p3_r"].at[0, dz], to)
        send(s2.at[base:], r3.at[dz, shared], s["p3_s"].at[1, dz], s["p3_r"].at[1, dz], to)
    mark("ar3_wait")
    mine = _at(z * 2 * w, 2 * w)
    acc = s2[mine, :]
    for dz in _peers(nz):
        arrived(r3.at[dz, own_units], s["p3_r"].at[0, dz])
        acc = acc + r3[dz, own_units, :]
    f2[mine, :] = acc
    for dz in _peers(nz):
        send(f2.at[mine], f2.at[mine], s["p4_s"].at[dz], s["p4_r"].at[nz - dz], dev(dz, 0, 0, c))
    acc_shared = s2[base:, :]
    for dz in _peers(nz):
        arrived(r3.at[dz, shared], s["p3_r"].at[1, dz])
        acc_shared = acc_shared + r3[dz, shared, :]
    lossb[c] = acc_shared[2 * rest :]
    send(lossb.at[c], lossb.at[c], s["ls_s"], s["ls_r"], sibling)
    mark("ar4_wait")
    for dz in _peers(nz):
        arrived(f2.at[_at(lax.rem(z + dz, nz) * 2 * w, 2 * w)], s["p4_r"].at[dz])
    for color in PAIR:
        start = color * HALF_ROWS + q1[color] * p.c1[color] + q2[color] * c2
        for i in range(nz):
            at = (2 * i + color) * w
            fin[c, _at(start + i * w, w), :] = f2[at : at + w, :]
        if rest:
            fin[c, _at(start + nz * w, rest), :] = acc_shared[color * rest : (color + 1) * rest]
        place = fin.at[c, _at(start, c2)]
        for d in _peers(p.n2[color]):
            send(place, place, s["p5_s"].at[color, d], s["p5_r"].at[color, p.n2[color] - d], along2(color, d))
    mark("ar5_wait")

    def chunk(color, tower_index, d):
        start = color * HALF_ROWS + lax.rem(q1[color] + d, p.n1[color]) * p.c1[color]
        return fin.at[tower_index, _at(start, p.c1[color])]

    def share(color, d):
        send(chunk(color, c, d), chunk(color, c, d), s["sb_s"].at[color, d], s["sb_r"].at[color, d], sibling)

    for color in PAIR:
        n1, n2 = p.n1[color], p.n2[color]
        for d in _peers(n2):
            start = color * HALF_ROWS + q1[color] * p.c1[color] + lax.rem(q2[color] + d, n2) * c2
            arrived(fin.at[c, _at(start, c2)], s["p5_r"].at[color, d])
        place = chunk(color, c, 0)
        for d in _peers(n1):
            send(place, place, s["p6_s"].at[color, d], s["p6_r"].at[color, n1 - d], along1(color, d))
        share(color, 0)
    mark("ar6_wait")
    for d in _peers(max(p.n1)):
        for color in PAIR:
            if d < p.n1[color]:
                arrived(chunk(color, c, d), s["p6_r"].at[color, d])
                share(color, d)
    mark("sib_wait")
    arrived(lossb.at[1 - c], s["ls_r"])
    loss[...] = jnp.sum(lossb[0] + lossb[1], axis=1, keepdims=True)[:1] * inv_batch + jnp.zeros(loss.shape, F32)
    for d in range(max(p.n1)):
        for color in PAIR:
            if d < p.n1[color]:
                arrived(chunk(color, 1 - c, d), s["sb_r"].at[color, d])

    mark("final_waits")
    for i, (ref, n) in enumerate(((idb, n_small), (lqb, n_small), (idq, nz - 1))):
        if n:
            pltpu.make_async_copy(ref.at[pl.ds(0, n)], ref.at[pl.ds(0, n)], sm_s.at[i]).wait()

    def left(ref, sem):
        rcopy(ref, ref, sem, sem, sibling).wait_send()

    def sent(k, _):
        left(vpart(k, lane), s["fw_s"].at[k])
        left(dvo.at[k], s["do_s"].at[k])
        left(dvs.at[k], s["dv_s"].at[k])
        return 0

    lax.fori_loop(1, npl, sent, 0)
    left(dvs.at[0], s["dv_s"].at[0])
    for cp in sends:
        cp.wait_send()
    mark()


def _layout_kernel(fin, loss_in, *refs):
    outs, sem = refs[:-1], refs[-1]
    copies = []

    def put(src, dst):
        cp = pltpu.make_async_copy(src, dst, sem.at[len(copies)])
        cp.start()
        copies.append(cp)

    for t in PAIR:
        o1, o2, o3 = outs[COLS * t : COLS * (t + 1)]
        for j in range(COLS):
            put(fin.at[t, W_IN * j : W_IN * (j + 1)], o1.at[:, _lanes(j)])
            put(fin.at[t, AT_2 + W_A * j : AT_2 + W_A * (j + 1)], o2.at[:, _lanes(j)])
        put(fin.at[t, AT_3:], o3)
    outs[-1][0, 0] = jnp.max(loss_in[...])
    for cp in copies:
        cp.wait()


def _step(p, ux, ix, ids, lq, uw1, uw2, uw3, iw1, iw2, iw3):
    scratch = _scratch(p)
    anywhere, vmem = pl.BlockSpec(memory_space=pl.ANY), pl.BlockSpec(memory_space=pltpu.VMEM)
    fin, loss = pl.pallas_call(
        functools.partial(_kernel, p, tuple(scratch)),
        out_shape=(pltpu.VMEM((2, GRAD_ROWS, L), F32), pltpu.VMEM((SUB, L), F32)),
        in_specs=[anywhere] * len((ux, ix, ids, lq, uw1, uw2, uw3, iw1, iw2, iw3)),
        out_specs=(vmem, vmem),
        scratch_shapes=list(scratch.values()),
        compiler_params=pltpu.CompilerParams(collective_id=0, has_side_effects=True, vmem_limit_bytes=VMEM_BYTES),
        name="two_tower_step",
    )(ux, ix, ids.reshape(1, L), lq.reshape(1, L), uw1, uw2, uw3, iw1, iw2, iw3)
    shapes = [(W_IN, W_A), (W_A, W_B), (W_B, L)] * 2
    *grads, loss = pl.pallas_call(
        _layout_kernel,
        out_shape=[jax.ShapeDtypeStruct(a, F32) for a in [*shapes, (1, 1)]],
        in_specs=[vmem, vmem],
        out_specs=[anywhere] * len(shapes) + [pl.BlockSpec(memory_space=pltpu.SMEM)],
        scratch_shapes=[pltpu.SemaphoreType.DMA((2 * (2 * COLS + 1),))],
        compiler_params=pltpu.CompilerParams(vmem_limit_bytes=LAYOUT_BYTES),
        name="layout",
    )(fin, loss)
    return (loss.reshape(()), *grads)


def solution(mesh):
    p = _Plan(mesh.shape["dp"])
    rows, vec, whole = P("dp", None), P("dp"), P()
    return jax.shard_map(
        functools.partial(_step, p),
        mesh=mesh,
        in_specs=(rows, rows, vec, vec, whole, whole, whole, whole, whole, whole),
        out_specs=(whole,) * (1 + 2 * COLS),
        check_vma=False,
    )
```

time: 1800 us -> 97.5 us (0.05)
  waiting for transfers between devices: 1480 us -> 0 us
  blocking collectives: 231 us -> 0 us
  Pallas kernels: 0 us -> 96.7 us
  matrix products: 44 us -> 0 us
  other arithmetic: 19.6 us -> 0 us
    reduce_scatter x1 -> x0, waiting for transfers between devices: 1290 us -> none  [device_step(): lax.psum_scatter(item_part, 'dp', scatter_dimension=0, tiled=True)]
    psum x1 -> x0, waiting for transfers between devices: 191 us -> none  [device_step(): lax.psum((jnp.sum(log_norm - pos_score),) + user_grads + item_grads, 'dp')]
    all_gather x2 -> x0, blocking collectives: 151 us -> none  [the longest x1 79 us: device_step(): logq_all = lax.all_gather(log_q, 'dp', axis=0, tiled=True)]
    pallas_call x0 -> x2, Pallas kernels: none -> 96.7 us  [the longest x1 94.7 us: _step(): pl.pallas_call(functools.partial(_kernel, p, tuple(scratch)), out_shape=(...]
    psum x1 -> x0, blocking collectives: 80.2 us -> none  [device_step(): lax.psum((jnp.sum(log_norm - pos_score),) + user_grads + item_grads, 'dp')]
    dot_general x17 -> x0, matrix products: 44 us -> none  [the longest x1 13.4 us: device_step(): lax.dot_general(user_half, item_all, COL_DIMS, preferred_element_type=jnp...]
  transfers between devices with their start and end apart: 3 -> 0, of which waited for: 2 -> 0; matrix products, arithmetic and copies ran while one was open for 1% -> 0% of each run, Pallas kernels for 0% -> 0%
where the time goes in v1:
time: 97.5 us; the launch traced here: 97.4 us
  Pallas kernels  96.7 us (99%)
    pallas_call x1, Pallas kernels, _step(): pl.pallas_call(functools.partial(_kernel, p, tuple(scratch)), out_shape=(...  94.7 us
    pallas_call x1, Pallas kernels, _step(): pl.pallas_call(_layout_kernel, out_shape=[jax.ShapeDtypeStruct(a, F32) fo...  2.03 us

profile of v1, /device:TPU:1, one launch (start us, length us, event | category | flops | bytes accessed | tf_op | source)
XLA Modules:
  0.0 97.4 jit_solution(7813682933656593193)
XLA Ops:
  0.6 94.7 %two_tower_step.1 = (f32[2,2304,128]{2,1,0:T(8,128)S(1)}, f32[8,128]{1,0:T(8,128)S(1)}) custom-call(f32[128,256]{1,0:T(8,128)} %ux.1, f32[128,256]{1,0:T(8,128)} %ix.1, s32[1,128]{1,0:T(1,128)} %bitcast.3, f32[1,128]{1,0:T(1,128)} %bitcast.4, f32[256,384]{1,0:T(8,128)} %uw1.1, f32[384,384]{1,0:T(8,128)} %uw2.1, f32[384,128]{1,0:T(8,128)} %uw3.1, ...), custom_call_target="tpu_custom_call" | custom-call | tf_op jit(solution)/shard_map/two_tower_step/pallas_call | solution.py:736
  95.3 2.0 %layout.1 = (f32[256,384]{1,0:T(8,128)}, f32[384,384]{1,0:T(8,128)}, f32[384,128]{1,0:T(8,128)}, f32[256,384]{1,0:T(8,128)}, f32[384,384]{1,0:T(8,128)}, /*index=5*/f32[384,128]{1,0:T(8,128)}, f32[1,1]{1,0:T(1,128)}) custom-call(f32[2,2304,128]{2,1,0:T(8,128)S(1)} %get-tuple-element.16.fin, f32[8,128]{1,0:T(8,128)S(1)} %get-tuple-element.17.loss_in), custom_call_target="tpu_custom_call" | custom-call | tf_op jit(solution)/shard_map/layout/pallas_call | solution.py:746

commit v2 on v1

v2 whole, which is shorter than its diff:
```python
import functools
import math

import jax
import jax.numpy as jnp
from jax import lax
from jax.experimental import pallas as pl
from jax.experimental.pallas import tpu as pltpu
from jax.sharding import PartitionSpec as P

F32, BF16, I32 = jnp.float32, jnp.bfloat16, jnp.int32
MESH = pl.DeviceIdType.MESH

GRID = {256: (8, 4, 4)}

L, SUB = 128, 8
PAIR = range(2)
USER, ITEM = PAIR
W_IN, W_A, W_B = 256, 384, 384
DUO = 2 * L
MAX_GROUPS = 32
TEMP = 0.05
INV_TEMP = 1.0 / TEMP
EXP_SCALE = INV_TEMP * math.log2(math.e)
NORM_EPS = 1e-6
LOW = -3.0e38
ROWS_1, ROWS_2, ROWS_3 = W_IN * W_A // L, W_A * W_B // L, W_B
AT_3, AT_2, AT_1 = 0, ROWS_3, ROWS_3 + ROWS_2
GRAD_ROWS = AT_1 + ROWS_1
STREAM, STREAM_C = 512, 256
AT_C = 2 * STREAM
STREAMS = (0, STREAM, AT_C + STREAM_C, AT_C + STREAM_C + STREAM)
COLS = W_A // L
X_AT, H1_AT, H2_AT, ACT_ROWS = 0, W_IN, W_IN + W_A, W_IN + W_A + W_B
GROUP = 4
VMEM_BYTES, LAYOUT_BYTES = 56 << 20, 1 << 20
NN = (((1,), (0,)), ((), ()))
NT = (((1,), (1,)), ((), ()))


def _dot(a, b, dims=NN):
    return lax.dot_general(a, b, dims, preferred_element_type=F32)


def _near(k):
    return k + k // 2 - 2 * (k // 3)


def _lanes(j, n=1):
    return slice(j * L, (j + n) * L)


def _at(start, size):
    return pl.ds(pl.multiple_of(start, SUB), size)


def _peers(n):
    return range(1, n)


def _iota(shape, dim):
    return lax.broadcasted_iota(I32, shape, dim)


class _Marks:
    def __init__(self):
        self.scope = None

    def __call__(self, name=None):
        if self.scope is not None:
            self.scope.__exit__(None, None, None)
        self.scope = jax.named_scope(name) if name else None
        if name:
            self.scope.__enter__()


class _Plan:
    def __init__(self, n):
        nz, ny, nx = self.nz, self.ny, self.nx = GRID[n]
        self.plane = nx * ny
        self.batch = n * L
        self.queries = nz * L
        self.ch1 = tuple(STREAM // m for m in (nx, ny))
        self.ch2 = STREAM // self.plane
        self.zc = 2 * self.ch2 // nz
        self.cz = STREAM_C // nz
        self.cx = self.cz // nx
        self.offsets = [(_near(k // nx), _near(k % nx)) for k in range(self.plane)]
        self.zorder = sorted(range(nz), key=lambda d: -min(d, nz - d))
        self.own = self.zorder.index(0)

    def slot(self, dy, dx):
        return self.offsets.index((dy % self.ny, dx % self.nx))

    def tile(self, dz):
        return self.zorder.index(dz % self.nz)


def _scratch(p):
    npl, nz, nq = p.plane, p.nz, p.queries
    vm, dma = pltpu.VMEM, pltpu.SemaphoreType.DMA
    groups, most = 2 * npl, max(p.nx, p.ny)
    nrx = max(groups, 2 * nz)
    chunk = max(p.ch1)
    items = npl * DUO
    return dict(
        xs=vm((2, L, W_IN), F32),
        wf1=vm((2, W_IN, W_A), F32),
        wf2=vm((2, W_A, W_B), F32),
        wf3=vm((2, W_B, L), F32),
        w2=vm((2, W_A, W_B), BF16),
        w3=vm((2, W_B, L), BF16),
        acts=vm((2, ACT_ROWS, DUO), BF16),
        hid=vm((2, DUO, W_A + W_B), BF16),
        unit=vm((2, DUO, DUO), F32),
        idb=vm((groups, 1, L), I32),
        lqb=vm((groups, 1, L), F32),
        idq=vm((nz, 1, L), I32),
        idk=vm((MAX_GROUPS, L), I32),
        lqk=vm((MAX_GROUPS, L), F32),
        idc=vm((items, L), I32),
        vaug=vm((items, DUO), BF16),
        vt=vm((L, items), BF16),
        uall=vm((nq, L), BF16),
        ut=vm((DUO, nq), BF16),
        tb=vm((items, nq), F32),
        ls=vm((SUB, nq), F32),
        dg=vm((1, L), F32),
        stat=vm((nz, 2, nq), F32),
        fac=vm((2, nq), F32),
        gt=vm((items, nq), BF16),
        dvp=vm((items, L), F32),
        dvs=vm((npl, L, L), F32),
        dvo=vm((npl, L, L), F32),
        dut=vm((nz, L, L), F32),
        rx=vm((nrx, L, L), F32),
        de=vm((DUO, L), F32),
        g=vm((GRAD_ROWS, L), F32),
        gc=vm((nz * (p.cz + SUB), L), F32),
        r1=vm((4, most, chunk, L), F32),
        s1=vm((4, chunk, L), F32),
        r2=vm((4, most, p.ch2, L), F32),
        s2=vm((2, 2 * p.ch2, L), F32),
        r3=vm((2, nz, p.zc, L), F32),
        rc1=vm((nz, p.cz + SUB, L), F32),
        sc1=vm((p.cz + SUB, L), F32),
        rc2=vm((p.nx, p.cx + SUB, L), F32),
        rc3=vm((p.ny, p.cx + SUB, L), F32),
        lossb=vm((2, SUB, L), F32),
        ld=dma((3 + 2 * 4,)),
        sm_s=dma((3,)),
        sm_r=dma((3,)),
        v_s=dma((npl,)),
        v_r=dma((npl,)),
        fw_s=dma((npl,)),
        fw_r=dma((npl,)),
        u_s=dma((nz,)),
        u_r=dma((nz,)),
        ac_s=dma((3,)),
        ac_r=dma((3,)),
        st_s=dma((nz,)),
        st_r=dma((nz,)),
        dv_s=dma((npl,)),
        dv_r=dma((npl,)),
        do_s=dma((npl,)),
        du_s=dma((nz,)),
        rx_r=dma((nrx,)),
        p1_s=dma((4, most)),
        p1_r=dma((4, most)),
        p2_s=dma((4, most)),
        p2_r=dma((4, most)),
        p3_s=dma((2, nz)),
        p3_r=dma((2, nz)),
        p4_s=dma((2, nz)),
        p4_r=dma((2, nz)),
        p5_s=dma((4, most)),
        p5_r=dma((4, most)),
        p6_s=dma((4, most)),
        p6_r=dma((4, most)),
        sb_s=dma((4 + 1, most)),
        sb_r=dma((4 + 1, most)),
        c1_s=dma((nz,)),
        c1_r=dma((nz,)),
        c2_s=dma((2, p.nx)),
        c2_r=dma((2, p.nx)),
        c3_s=dma((p.ny,)),
        c3_r=dma((p.ny,)),
        c4_s=dma((p.nx,)),
        c4_r=dma((p.nx,)),
        c5_s=dma((nz,)),
        c5_r=dma((nz,)),
        ls_s=dma(()),
        ls_r=dma(()),
    )


def _kernel(p, names, ux, ix, ids, lq, uw1, uw2, uw3, iw1, iw2, iw3, fin, loss, *refs):
    s = dict(zip(names, refs, strict=True))
    nz, ny, nx, npl, nq = p.nz, p.ny, p.nx, p.plane, p.queries
    half = nz // 2
    mark = _Marks()
    me = lax.axis_index("dp")
    c = lax.rem(me, 2)
    chip = lax.div(me, 2)
    x = lax.rem(chip, nx)
    y = lax.rem(lax.div(chip, nx), ny)
    z = lax.div(chip, nx * ny)
    sibling = me + 1 - 2 * c

    def dev(dz, dy, dx, core):
        zz, yy, xx = lax.rem(z + dz, nz), lax.rem(y + dy, ny), lax.rem(x + dx, nx)
        return ((zz * ny + yy) * nx + xx) * 2 + core

    def rcopy(src, dst, send, recv, to):
        return pltpu.make_async_remote_copy(
            src_ref=src, dst_ref=dst, send_sem=send, recv_sem=recv, device_id=(to,), device_id_type=MESH
        )

    sends = []

    def send(src, dst, ssem, rsem, to):
        cp = rcopy(src, dst, ssem, rsem, to)
        cp.start()
        sends.append(cp)

    def arrived(dst, rsem):
        rcopy(dst, dst, rsem, rsem, me).wait_recv()

    lane = pl.ds(pl.multiple_of(c * L, L), L)
    other = pl.ds(pl.multiple_of((1 - c) * L, L), L)

    mark("start")
    xs, idb, lqb, idq, ld = s["xs"], s["idb"], s["lqb"], s["idq"], s["ld"]
    own = p.own
    small = [(ids, idb.at[c]), (lq, lqb.at[c]), (ids, idq.at[own])]
    small = [pltpu.make_async_copy(a, b, ld.at[i]) for i, (a, b) in enumerate(small)]
    loads = {}
    n_ld = len(small)
    for t, given in ((ITEM, (ix, iw1, iw2, iw3)), (USER, (ux, uw1, uw2, uw3))):
        loads[t] = []
        for src, dst in zip(given, (xs, s["wf1"], s["wf2"], s["wf3"]), strict=True):
            loads[t].append(pltpu.make_async_copy(src, dst.at[t], ld.at[n_ld]))
            n_ld += 1
    for cp in small + loads[ITEM] + loads[USER]:
        cp.start()

    barrier = pltpu.get_barrier_semaphore()
    others = [dev(0, dy, dx, core) for core in PAIR for dy, dx in p.offsets[1:]]
    others += [dev(dz, 0, 0, core) for core in PAIR for dz in _peers(nz)]
    others.append(sibling)
    for to in others:
        pl.semaphore_signal(barrier, inc=1, device_id=(to,), device_id_type=MESH)

    acts, hid, unit = s["acts"], s["hid"], s["unit"]

    def tower(t):
        place = jnp.where(c == t, 0, 1)
        for cp in loads[t]:
            cp.wait()
        w1, w2, w3 = s["wf1"][t].astype(BF16), s["wf2"][t].astype(BF16), s["wf3"][t].astype(BF16)
        s["w2"][t], s["w3"][t] = w2, w3
        xh = xs[t].astype(BF16)
        h1 = jnp.maximum(_dot(xh, w1), 0.0).astype(BF16)
        h2 = jnp.maximum(_dot(h1, w2), 0.0).astype(BF16)
        raw = _dot(h2, w3)
        inv = lax.rsqrt(jnp.sum(raw * raw, axis=1, keepdims=True) + NORM_EPS)
        e = raw * inv
        acts[place, X_AT:H1_AT, lane] = xh.T
        acts[place, H1_AT:H2_AT, lane] = h1.T
        acts[place, H2_AT:ACT_ROWS, lane] = h2.T
        hid[place, lane, :W_A] = h1
        hid[place, lane, W_A:] = h2
        unit[place, lane, :L] = e
        unit[place, lane, L:] = jnp.broadcast_to(inv, (L, L))
        return e.astype(BF16)

    mark("towers")
    vaug, uall = s["vaug"], s["uall"]
    vaug[lane, :L] = tower(ITEM)
    uall[_lanes(own), :] = tower(USER)
    for cp in small:
        cp.wait()
    mark("barrier_wait")
    pl.semaphore_wait(barrier, len(others))

    mark("send_uv")
    sm_s, sm_r = s["sm_s"], s["sm_r"]

    def send_small(k, to):
        rcopy(idb.at[c], idb.at[2 * k + c], sm_s.at[0], sm_r.at[0], to).start()
        rcopy(lqb.at[c], lqb.at[2 * k + c], sm_s.at[1], sm_r.at[1], to).start()

    send_small(0, sibling)
    for dy, dx in p.offsets[1:]:
        for core in PAIR:
            send_small(p.slot(-dy, -dx), dev(0, dy, dx, core))
    n_small = 2 * npl - 1
    for dz in _peers(nz):
        rcopy(idq.at[own], idq.at[p.tile(-dz)], sm_s.at[2], sm_r.at[2], dev(dz, 0, 0, c)).start()

    def vpart(k, core):
        return vaug.at[pl.ds(pl.multiple_of(k * DUO + core * L, L), L), pl.ds(0, L)]

    def upart(j):
        return uall.at[_lanes(j)]

    send(vpart(0, c), vpart(0, c), s["fw_s"].at[0], s["fw_r"].at[0], sibling)
    for i in range(1, max(npl, nz)):
        if i < nz:
            dz = p.zorder[-1 - i]
            send(upart(own), upart(p.tile(-dz)), s["u_s"].at[dz], s["u_r"].at[p.tile(-dz)], dev(dz, 0, 0, c))
        if i < npl:
            dy, dx = p.offsets[i]
            k = p.slot(-dy, -dx)
            send(vpart(0, c), vpart(k, c), s["v_s"].at[i], s["v_r"].at[k], dev(0, dy, dx, c))
    for i, part in enumerate(((acts, slice(None), lane), (hid, lane, slice(None)), (unit, lane, slice(None)))):
        ref, rows, cols = part
        send(ref.at[1, rows, cols], ref.at[0, rows, cols], s["ac_s"].at[i], s["ac_r"].at[i], sibling)

    mark("small_wait")
    idk, lqk, idc, ut = s["idk"], s["lqk"], s["idc"], s["ut"]
    idk[...] = jnp.full(idk.shape, -1, I32)
    lqk[...] = jnp.full(lqk.shape, -LOW, F32)
    ut[L:, :] = jnp.where(_iota((L, nq), 0) < 3 * MAX_GROUPS, -1.0, 0.0).astype(BF16)
    for i, (ref, n) in enumerate(((idb, n_small), (lqb, n_small), (idq, nz - 1))):
        if n:
            pltpu.make_async_copy(ref.at[pl.ds(0, n)], ref.at[pl.ds(0, n)], sm_r.at[i]).wait()
    mark("turn")
    for g in range(2 * npl):
        row = idb[g]
        idk[g : g + 1, :] = row
        lqk[g : g + 1, :] = lqb[g] * TEMP
        idc[_lanes(g), :] = jnp.broadcast_to(row, (L, L)).T

    def parts(q):
        hi = q.astype(BF16).astype(F32)
        mid = (q - hi).astype(BF16).astype(F32)
        return hi, mid, (q - hi - mid).astype(BF16).astype(F32)

    q_all, id_all = lqk[...], idk[...]
    split = parts(jnp.where(id_all < 0, 0.0, q_all))
    turned = jnp.concatenate([*split, jnp.zeros((MAX_GROUPS, L), F32)], axis=0).T.astype(BF16)
    col = _iota((L, L), 1)
    ones = jnp.where(col < 3 * MAX_GROUPS + 3, 1.0, 0.0)
    for g in range(2 * npl):
        keep = jnp.where(col < 3 * MAX_GROUPS, jnp.where(lax.rem(col, MAX_GROUPS) == g, turned.astype(F32), 0.0), ones)
        vaug[_lanes(g), L:] = keep.astype(BF16)

    def most(a):
        return jnp.max(jnp.max(a, axis=0, keepdims=True), axis=1, keepdims=True)

    top1 = most(-q_all)
    at_top = -q_all == top1
    id_hi, id_lo = (id_all // (1 << 16)).astype(F32), (id_all % (1 << 16)).astype(F32)
    top_hi = most(jnp.where(at_top, id_hi, -1.0))
    top_lo = most(jnp.where(jnp.logical_and(at_top, id_hi == top_hi), id_lo, -1.0))
    same_top = jnp.logical_and(id_hi == top_hi, id_lo == top_lo)
    top2 = most(jnp.where(same_top, LOW, -q_all))
    top2 = jnp.where(top2 <= LOW, top1, top2)
    id_top = top_hi.astype(I32) * (1 << 16) + top_lo.astype(I32)
    stat = s["stat"]
    bounds = []
    for j in range(nz):
        rest = top2
        if j == own:
            rest = jnp.maximum(top2, -lqb[c] * TEMP)
        bounds.append(jnp.where(idq[j] == id_top, rest, jnp.broadcast_to(top1, (1, L))))
    bound = jnp.concatenate(bounds, axis=1)
    stat[0, :1, :] = bound
    at = L + 3 * MAX_GROUPS
    ut[at : at + 16, :] = jnp.concatenate([-a for a in parts(bound)] + [jnp.zeros((16 - 3, nq), F32)], axis=0).astype(BF16)

    tb, ls, vt, dg = s["tb"], s["ls"], s["vt"], s["dg"]
    ls[...] = jnp.zeros(ls.shape, F32)
    diag = _iota((DUO, L), 0) == _iota((DUO, L), 1) + c * L
    far, close = range(half), range(half, nz)

    def queries(tiles):
        for j in reversed(tiles):
            if j != own:
                arrived(upart(j), s["u_r"].at[j])
            ut[:L, _lanes(j)] = uall[_lanes(j), :].T

    def pass1(blocks, tiles):
        rows = slice(blocks[0] * DUO, (blocks[-1] + 1) * DUO)
        wide = _dot(vaug[rows, :], ut[:, _lanes(tiles[0], len(tiles))])
        for i, r in enumerate(tiles):
            add = 0.0
            for n, k in enumerate(blocks):
                at = slice(k * DUO, (k + 1) * DUO)
                t = wide[n * DUO : (n + 1) * DUO, _lanes(i)]
                drop = idc[at, :] == idq[r]
                if k == 0 and r == own:
                    drop = jnp.logical_and(drop, jnp.logical_not(diag))
                    dg[...] = jnp.sum(jnp.where(diag, t, 0.0), axis=0, keepdims=True)
                e = jnp.where(drop, 0.0, jnp.exp2(t * EXP_SCALE))
                tb[at, _lanes(r)] = e
                add = add + jnp.sum(e.reshape(DUO // SUB, SUB, L), axis=0)
            ls[:, _lanes(r)] += add

    def forward(blocks):
        for k in blocks:
            if k:
                arrived(vpart(k, c), s["v_r"].at[k])
                send(vpart(k, c), vpart(k, c), s["fw_s"].at[k], s["fw_r"].at[k], sibling)

    def whole(blocks):
        for k in blocks:
            arrived(vpart(k, 1 - c), s["fw_r"].at[k])

    size = min(GROUP, npl)
    groups = [range(a, a + size) for a in range(0, npl, size)]
    early = groups[: len(groups) // 2]
    late = groups[len(early) :]
    mark("u_close")
    queries(close)
    mark("pass1_close")
    forward(groups[0])
    for n, blocks in enumerate(early):
        forward(groups[n + 1])
        whole(blocks)
        pass1(blocks, close)
    mark("u_far")
    queries(far)
    mark("pass1_far")
    for blocks in early:
        pass1(blocks, far)
    mark("pass1_late")
    for n, blocks in enumerate(late):
        if n + 1 < len(late):
            forward(late[n + 1])
        whole(blocks)
        pass1(blocks, close)
        pass1(blocks, far)

    mark("stat_send")
    stat[0, 1:, :] = jnp.sum(ls[...], axis=0, keepdims=True)
    for dz in _peers(nz):
        send(stat.at[0], stat.at[nz - dz], s["st_s"].at[dz], s["st_r"].at[nz - dz], dev(dz, 0, 0, c))

    for k in range(2 * npl):
        vt[:, _lanes(k)] = vaug[_lanes(k), :L].T
    mark("stat_wait")
    for dz in _peers(nz):
        arrived(stat.at[dz], s["st_r"].at[dz])

    def theirs(row, dz):
        a = stat[dz, row : row + 1, :]
        return a if dz == 0 else jnp.concatenate([a[:, _lanes(p.tile(d - dz))] for d in p.zorder], axis=1)

    sums = [theirs(1, dz) for dz in range(nz)]
    tops = [jnp.where(a > 0.0, theirs(0, dz), LOW) for dz, a in enumerate(sums)]
    top = functools.reduce(jnp.maximum, tops)
    total = sum(a * jnp.exp2((b - top) * EXP_SCALE) for a, b in zip(sums, tops, strict=True))
    mine = _lanes(own)
    loss_part = (top[:, mine] - bound[:, mine] - dg[...]) * INV_TEMP + jnp.log(total[:, mine])
    loss_tile = jnp.where(_iota((SUB, L), 0) == 0, loss_part, 0.0)
    fac = s["fac"]
    inv_batch = 1.0 / p.batch
    fac[:1, :] = jnp.exp2((tops[0] - top) * EXP_SCALE) * (1.0 / total)
    fac[1:, :] = fac[:1, :] * inv_batch

    gt, dut, dvp, dvs, dvo, rx = s["gt"], s["dut"], s["dvp"], s["dvs"], s["dvo"], s["rx"]
    plane = y * nx + x

    def grads(blocks, tiles):
        for k in blocks:
            at = slice(k * DUO, (k + 1) * DUO)
            for r in tiles:
                if k == 0 and r == own:
                    g = (tb[at, _lanes(r)] * fac[:1, _lanes(r)] - jnp.where(diag, 1.0, 0.0)) * inv_batch
                else:
                    g = tb[at, _lanes(r)] * fac[1:, _lanes(r)]
                gt[at, _lanes(r)] = g.astype(BF16)

    def user_part(blocks, tiles, first):
        rows = slice(blocks[0] * DUO, (blocks[-1] + 1) * DUO)
        part = _dot(vt[:, rows], gt[rows, _lanes(tiles[0], len(tiles))])
        for i, r in enumerate(tiles):
            piece = part[:, _lanes(i)]
            dut[r] = piece if first else dut[r] + piece

    def item_part(blocks):
        rows = slice(min(blocks) * DUO, (max(blocks) + 1) * DUO)
        dvp[rows, :] = _dot(gt[rows, :], uall[...])
        for k in blocks:
            src = dvp.at[pl.ds(pl.multiple_of(k * DUO + (1 - c) * L, L), L)]
            send(src, dvs.at[k], s["dv_s"].at[k], s["dv_r"].at[k], sibling)

    def send_du(tiles):
        for j in tiles:
            dz = p.zorder[j]
            if dz:
                send(dut.at[j], rx.at[2 * z + c], s["du_s"].at[dz], s["rx_r"].at[2 * z + c], dev(dz, 0, 0, 0))

    def finish(blocks):
        for k in blocks:
            arrived(dvs.at[k], s["dv_r"].at[k])
            dvo[k] = dvp[pl.ds(pl.multiple_of(k * DUO + c * L, L), L), :] + dvs[k]
            if k:
                dy, dx = p.offsets[k]
                send(dvo.at[k], rx.at[2 * plane + c], s["do_s"].at[k], s["rx_r"].at[2 * plane + c], dev(0, dy, dx, 1))

    mark("pass2a")
    for n, blocks in enumerate(groups):
        grads(blocks, far)
        user_part(blocks, far, n == 0)
    send_du(far)
    mark("pass2b")
    order, lo = [], npl
    while lo:
        take = min(GROUP if len(order) > 1 else GROUP // 2, lo)
        order.append(range(lo - take, lo))
        lo -= take
    for n, blocks in enumerate(order):
        grads(blocks, close)
        item_part(blocks[::-1])
        user_part(blocks, close, n == 0)
        if n:
            finish(order[n - 1][::-1])
    mark("rs_send")
    send_du(close)
    finish(order[-1][::-1])

    mark("rs_wait")
    de = s["de"]

    def gather(h, acc, order, turn):
        for j in order:
            arrived(rx.at[j], s["rx_r"].at[j])
            acc = rx[j] if acc is None else acc + rx[j]
        de[_lanes(h), :] = (acc.T if turn else acc) * INV_TEMP

    z_from = [lax.rem(z + d, nz) for d in p.zorder if d]
    plane_from = [
        lax.rem(y + ny - dy, ny) * nx + lax.rem(x + nx - dx, nx) for dy, dx in reversed(p.offsets[1:])
    ]

    @pl.when(c == USER)
    def _():
        cp = rcopy(dvo.at[0], rx.at[2 * plane], s["do_s"].at[0], s["rx_r"].at[2 * plane], sibling)
        cp.start()
        gather(0, dut[own], [2 * a for a in z_from], True)
        gather(1, None, [2 * a + 1 for a in [*z_from, z]], True)
        cp.wait_send()

    @pl.when(c == ITEM)
    def _():
        cp = rcopy(dut.at[own], rx.at[2 * z + 1], s["du_s"].at[0], s["rx_r"].at[2 * z + 1], sibling)
        cp.start()
        gather(1, dvo[0], [2 * a + 1 for a in plane_from], False)
        gather(0, None, [2 * a for a in [*plane_from, plane]], False)
        cp.wait_send()

    mark("backward")
    arrived(acts.at[0, :, other], s["ac_r"].at[0])
    arrived(hid.at[0, other, :], s["ac_r"].at[1])
    arrived(unit.at[0, other, :], s["ac_r"].at[2])
    g, gc = s["g"], s["gc"]
    cz, cx, ch2, zc = p.cz, p.cx, p.ch2, p.zc
    stride_c = cz + SUB

    def put(start, val):
        n, done = val.shape[0], 0
        while done < n:
            row = start + done
            if AT_C <= row < AT_C + STREAM_C:
                chunk, off = (row - AT_C) // cz, (row - AT_C) % cz
                take = min(n - done, cz - off)
                to = chunk * stride_c + off
                gc[to : to + take, :] = val[done : done + take]
            else:
                take = n - done if row >= AT_C else min(n - done, AT_C - row)
                g[row : row + take, :] = val[done : done + take]
            done += take

    def toward(along_x, d):
        return dev(0, 0, d, c) if along_x else dev(0, d, 0, c)

    class Stream:
        def __init__(self, i):
            self.i, self.start = i, STREAMS[i]
            self.along_x = i % 2 == 0
            self.n1, self.n2 = (nx, ny) if self.along_x else (ny, nx)
            self.q1, self.q2 = (x, y) if self.along_x else (y, x)
            self.ch1 = STREAM // self.n1

        def to1(self, d):
            return toward(self.along_x, d)

        def to2(self, d):
            return toward(not self.along_x, d)

        def chunk1(self, d):
            return _at(self.start + lax.rem(self.q1 + d, self.n1) * self.ch1, self.ch1)

        def row2(self, d):
            return self.start + self.q1 * self.ch1 + lax.rem(self.q2 + d, self.n2) * ch2

        def sem(self, name, d):
            return s[name].at[self.i, d]

    streams = [Stream(i) for i in range(len(STREAMS))]
    sets = (streams[:2], streams[2:])
    r1, s1, r2, s2, r3, lossb = s["r1"], s["s1"], s["r2"], s["s2"], s["r3"], s["lossb"]
    rc1, sc1, rc2, rc3 = s["rc1"], s["sc1"], s["rc2"], s["rc3"]

    def phase1(pair):
        for d in _peers(max(nx, ny)):
            for st in pair:
                if d < st.n1:
                    send(g.at[st.chunk1(d)], r1.at[st.i, d, : st.ch1], st.sem("p1_s", d), st.sem("p1_r", d), st.to1(d))

    def phase2(pair):
        for st in pair:
            acc = g[st.chunk1(0), :]
            for d in _peers(st.n1):
                arrived(r1.at[st.i, d, : st.ch1], st.sem("p1_r", d))
                acc = acc + r1[st.i, d, : st.ch1, :]
            s1[st.i, : st.ch1, :] = acc
            for d in _peers(st.n2):
                at = _at(lax.rem(st.q2 + d, st.n2) * ch2, ch2)
                send(s1.at[st.i, at], r2.at[st.i, d], st.sem("p2_s", d), st.sem("p2_r", d), st.to2(d))

    def phase3(n, pair):
        for j, st in enumerate(pair):
            acc = s1[st.i, _at(st.q2 * ch2, ch2), :]
            for d in _peers(st.n2):
                arrived(r2.at[st.i, d], st.sem("p2_r", d))
                acc = acc + r2[st.i, d]
            s2[n, j * ch2 : (j + 1) * ch2, :] = acc
        for dz in _peers(nz):
            at = _at(lax.rem(z + dz, nz) * zc, zc)
            send(s2.at[n, at], r3.at[n, dz], s["p3_s"].at[n, dz], s["p3_r"].at[n, dz], dev(dz, 0, 0, c))

    def place(pair, dz):
        zz = lax.rem(z + dz, nz)
        second = lax.div(zz, nz // 2)
        first = pair[0].row2(0) * (1 - second) + pair[1].row2(0) * second
        return fin.at[c, _at(first + lax.rem(zz, nz // 2) * zc, zc)]

    def phase4(n, pair):
        acc = s2[n, _at(z * zc, zc), :]
        for dz in _peers(nz):
            arrived(r3.at[n, dz], s["p3_r"].at[n, dz])
            acc = acc + r3[n, dz]
        place(pair, 0)[...] = acc
        for dz in _peers(nz):
            send(place(pair, 0), place(pair, 0), s["p4_s"].at[n, dz], s["p4_r"].at[n, nz - dz], dev(dz, 0, 0, c))

    def phase5(n, pair):
        for dz in _peers(nz):
            arrived(place(pair, dz), s["p4_r"].at[n, dz])
        for st in pair:
            rows = fin.at[c, _at(st.row2(0), ch2)]
            for d in _peers(st.n2):
                send(rows, rows, st.sem("p5_s", d), st.sem("p5_r", st.n2 - d), st.to2(d))

    def share(rows, i, d):
        send(rows, rows, s["sb_s"].at[i, d], s["sb_r"].at[i, d], sibling)

    def phase6(pair):
        for st in pair:
            for d in _peers(st.n2):
                arrived(fin.at[c, _at(st.row2(d), ch2)], st.sem("p5_r", d))
            rows = fin.at[c, st.chunk1(0)]
            for d in _peers(st.n1):
                send(rows, rows, st.sem("p6_s", d), st.sem("p6_r", st.n1 - d), st.to1(d))
            share(rows, st.i, 0)

    def phase7(pair):
        for d in _peers(max(nx, ny)):
            for st in pair:
                if d < st.n1:
                    rows = fin.at[c, st.chunk1(d)]
                    arrived(rows, st.sem("p6_r", d))
                    share(rows, st.i, d)

    def step_c1():
        for dz in _peers(nz):
            at = _at(lax.rem(z + dz, nz) * stride_c, stride_c)
            send(gc.at[at], rc1.at[dz], s["c1_s"].at[dz], s["c1_r"].at[dz], dev(dz, 0, 0, c))

    def step_c2():
        acc = gc[_at(z * stride_c, stride_c), :]
        for dz in _peers(nz):
            arrived(rc1.at[dz], s["c1_r"].at[dz])
            acc = acc + rc1[dz]
        sc1[...] = acc
        for d in _peers(nx):
            at, to = _at(lax.rem(x + d, nx) * cx, cx), dev(0, 0, d, c)
            send(sc1.at[at], rc2.at[d, :cx], s["c2_s"].at[0, d], s["c2_r"].at[0, d], to)
            send(sc1.at[cz:], rc2.at[d, cx:], s["c2_s"].at[1, d], s["c2_r"].at[1, d], to)

    def step_c3():
        acc, loss_acc = sc1[_at(x * cx, cx), :], sc1[cz:, :]
        for d in _peers(nx):
            arrived(rc2.at[d, :cx], s["c2_r"].at[0, d])
            arrived(rc2.at[d, cx:], s["c2_r"].at[1, d])
            acc, loss_acc = acc + rc2[d, :cx, :], loss_acc + rc2[d, cx:, :]
        rc3[y, :cx, :] = acc
        rc3[y, cx:, :] = loss_acc
        for d in _peers(ny):
            send(rc3.at[y], rc3.at[y], s["c3_s"].at[d], s["c3_r"].at[ny - d], dev(0, d, 0, c))

    def rows_c(dz, d, size):
        return fin.at[c, _at(AT_C + lax.rem(z + dz, nz) * cz + lax.rem(x + d, nx) * (cx if size == cx else 0), size)]

    def step_c4():
        for d in _peers(ny):
            arrived(rc3.at[lax.rem(y + d, ny)], s["c3_r"].at[d])
        acc = rc3[0]
        for d in _peers(ny):
            acc = acc + rc3[d]
        rows = rows_c(0, 0, cx)
        rows[...] = acc[:cx]
        lossb[c] = acc[cx:]
        send(lossb.at[c], lossb.at[c], s["ls_s"], s["ls_r"], sibling)
        for d in _peers(nx):
            send(rows, rows, s["c4_s"].at[d], s["c4_r"].at[nx - d], dev(0, 0, d, c))

    def step_c5():
        for d in _peers(nx):
            arrived(rows_c(0, d, cx), s["c4_r"].at[d])
        rows = rows_c(0, 0, cz)
        for dz in _peers(nz):
            send(rows, rows, s["c5_s"].at[dz], s["c5_r"].at[nz - dz], dev(dz, 0, 0, c))

    whole_c = slice(AT_C, AT_C + STREAM_C)

    def step_c6():
        for dz in _peers(nz):
            arrived(rows_c(dz, 0, cz), s["c5_r"].at[dz])
        share(fin.at[c, whole_c], len(STREAMS), 0)

    for i in range(nz):
        gc[(i + 1) * stride_c - SUB : (i + 1) * stride_c, :] = loss_tile
    de_all = de[...]
    e, inv = unit[0, :, :L], unit[0, :, L:]
    dz_h = (inv * (de_all - e * jnp.sum(e * de_all, axis=1, keepdims=True))).astype(BF16)
    put(AT_3, _dot(acts[0, H2_AT:ACT_ROWS, :], dz_h))
    da2 = jnp.where(hid[0, :, W_A:] > 0, _dot(dz_h, s["w3"][c], NT), 0.0).astype(BF16)
    dw2 = _dot(acts[0, H1_AT:H2_AT, :], da2)
    for j in range(COLS):
        put(AT_2 + W_A * j, dw2[:, _lanes(j)])
    phase1(sets[0])
    step_c1()
    da1 = jnp.where(hid[0, :, :W_A] > 0, _dot(da2, s["w2"][c], NT), 0.0).astype(BF16)
    dw1 = _dot(acts[0, X_AT:H1_AT, :], da1)
    for j in range(COLS):
        put(AT_1 + W_IN * j, dw1[:, _lanes(j)])
    phase1(sets[1])

    for name, steps in (
        ("ar2", (phase2, phase2, step_c2)),
        ("ar3", (phase3, step_c3, phase3)),
        ("ar4", (phase4, step_c4, phase4)),
        ("ar5", (phase5, step_c5, phase5)),
        ("ar6", (phase6, phase6)),
        ("ar7", (step_c6, phase7, phase7)),
    ):
        n = 0
        for i, step in enumerate(steps):
            mark(f"{name}_{i}")
            if step in (phase2, phase6, phase7):
                step(sets[n])
                n += 1
            elif step in (phase3, phase4, phase5):
                step(n, sets[n])
                n += 1
            else:
                step()
    mark("sib_wait")
    arrived(lossb.at[1 - c], s["ls_r"])
    loss[...] = jnp.sum(lossb[0] + lossb[1], axis=1, keepdims=True)[:1] * inv_batch + jnp.zeros(loss.shape, F32)
    for pair in sets:
        for st in pair:
            for d in range(st.n1):
                arrived(fin.at[1 - c, st.chunk1(d)], s["sb_r"].at[st.i, d])
    arrived(fin.at[1 - c, whole_c], s["sb_r"].at[len(STREAMS), 0])

    mark("final_waits")
    for i, (ref, n) in enumerate(((idb, n_small), (lqb, n_small), (idq, nz - 1))):
        if n:
            pltpu.make_async_copy(ref.at[pl.ds(0, n)], ref.at[pl.ds(0, n)], sm_s.at[i]).wait()

    for cp in sends:
        cp.wait_send()
    mark()


def _layout_kernel(fin, loss_in, *refs):
    outs, sem = refs[:-1], refs[-1]
    copies = []

    def put(src, dst):
        cp = pltpu.make_async_copy(src, dst, sem.at[len(copies)])
        cp.start()
        copies.append(cp)

    for t in PAIR:
        o1, o2, o3 = outs[COLS * t : COLS * (t + 1)]
        for j in range(COLS):
            put(fin.at[t, AT_1 + W_IN * j : AT_1 + W_IN * (j + 1)], o1.at[:, _lanes(j)])
            put(fin.at[t, AT_2 + W_A * j : AT_2 + W_A * (j + 1)], o2.at[:, _lanes(j)])
        put(fin.at[t, AT_3:AT_2], o3)
    outs[-1][0, 0] = jnp.max(loss_in[...])
    for cp in copies:
        cp.wait()


def _step(p, ux, ix, ids, lq, uw1, uw2, uw3, iw1, iw2, iw3):
    scratch = _scratch(p)
    anywhere, vmem = pl.BlockSpec(memory_space=pl.ANY), pl.BlockSpec(memory_space=pltpu.VMEM)
    fin, loss = pl.pallas_call(
        functools.partial(_kernel, p, tuple(scratch)),
        out_shape=(pltpu.VMEM((2, GRAD_ROWS, L), F32), pltpu.VMEM((SUB, L), F32)),
        in_specs=[anywhere] * len((ux, ix, ids, lq, uw1, uw2, uw3, iw1, iw2, iw3)),
        out_specs=(vmem, vmem),
        scratch_shapes=list(scratch.values()),
        compiler_params=pltpu.CompilerParams(collective_id=0, has_side_effects=True, vmem_limit_bytes=VMEM_BYTES),
        name="two_tower_step",
    )(ux, ix, ids.reshape(1, L), lq.reshape(1, L), uw1, uw2, uw3, iw1, iw2, iw3)
    shapes = [(W_IN, W_A), (W_A, W_B), (W_B, L)] * 2
    *grads, loss = pl.pallas_call(
        _layout_kernel,
        out_shape=[jax.ShapeDtypeStruct(a, F32) for a in [*shapes, (1, 1)]],
        in_specs=[vmem, vmem],
        out_specs=[anywhere] * len(shapes) + [pl.BlockSpec(memory_space=pltpu.SMEM)],
        scratch_shapes=[pltpu.SemaphoreType.DMA((2 * (2 * COLS + 1),))],
        compiler_params=pltpu.CompilerParams(vmem_limit_bytes=LAYOUT_BYTES),
        name="layout",
    )(fin, loss)
    return (loss.reshape(()), *grads)


def solution(mesh):
    p = _Plan(mesh.shape["dp"])
    rows, vec, whole = P("dp", None), P("dp"), P()
    return jax.shard_map(
        functools.partial(_step, p),
        mesh=mesh,
        in_specs=(rows, rows, vec, vec, whole, whole, whole, whole, whole, whole),
        out_specs=(whole,) * (1 + 2 * COLS),
        check_vma=False,
    )
```

time: 97.5 us -> 87.7 us (0.90)
  Pallas kernels: 96.7 us -> 86.8 us
    pallas_call x1, Pallas kernels: 94.7 us -> 84.8 us  [_step(): pl.pallas_call(functools.partial(_kernel, p, tuple(scratch)), out_shape=(...]
where the time goes in v2:
time: 87.7 us; the launch traced here: 87.6 us
  Pallas kernels  86.8 us (99%)
    pallas_call x1, Pallas kernels, _step(): pl.pallas_call(functools.partial(_kernel, p, tuple(scratch)), out_shape=(...  84.8 us
    pallas_call x1, Pallas kernels, _step(): pl.pallas_call(_layout_kernel, out_shape=[jax.ShapeDtypeStruct(a, F32) fo...  2.03 us

profile of v2, /device:TPU:1, one launch (start us, length us, event | category | flops | bytes accessed | tf_op | source)
XLA Modules:
  0.0 87.6 jit_solution(13077837008792926174)
XLA Ops:
  0.6 84.8 %two_tower_step.1 = (f32[2,2304,128]{2,1,0:T(8,128)S(1)}, f32[8,128]{1,0:T(8,128)S(1)}) custom-call(f32[128,256]{1,0:T(8,128)} %ux.1, f32[128,256]{1,0:T(8,128)} %ix.1, s32[1,128]{1,0:T(1,128)} %bitcast.3, f32[1,128]{1,0:T(1,128)} %bitcast.4, f32[256,384]{1,0:T(8,128)} %uw1.1, f32[384,384]{1,0:T(8,128)} %uw2.1, f32[384,128]{1,0:T(8,128)} %uw3.1, ...), custom_call_target="tpu_custom_call" | custom-call | tf_op jit(solution)/shard_map/two_tower_step/pallas_call | solution.py:815
  85.5 2.0 %layout.1 = (f32[256,384]{1,0:T(8,128)}, f32[384,384]{1,0:T(8,128)}, f32[384,128]{1,0:T(8,128)}, f32[256,384]{1,0:T(8,128)}, f32[384,384]{1,0:T(8,128)}, /*index=5*/f32[384,128]{1,0:T(8,128)}, f32[1,1]{1,0:T(1,128)}) custom-call(f32[2,2304,128]{2,1,0:T(8,128)S(1)} %get-tuple-element.16.fin, f32[8,128]{1,0:T(8,128)S(1)} %get-tuple-element.17.loss_in), custom_call_target="tpu_custom_call" | custom-call | tf_op jit(solution)/shard_map/layout/pallas_call | solution.py:825

commit v3 on v2

--- a/solution.py
+++ b/solution.py
@@ -33,6 +33,7 @@
 COLS = W_A // L
 X_AT, H1_AT, H2_AT, ACT_ROWS = 0, W_IN, W_IN + W_A, W_IN + W_A + W_B
 GROUP = 4
+LAG = 1
 VMEM_BYTES, LAYOUT_BYTES = 56 << 20, 1 << 20
 NN = (((1,), (0,)), ((), ()))
 NT = (((1,), (1,)), ((), ()))
@@ -86,21 +87,16 @@
         self.cz = STREAM_C // nz
         self.cx = self.cz // nx
         self.offsets = [(_near(k // nx), _near(k % nx)) for k in range(self.plane)]
-        self.zorder = sorted(range(nz), key=lambda d: -min(d, nz - d))
-        self.own = self.zorder.index(0)
+        self.evens = sorted(range(0, nz, 2), key=lambda d: -min(d, nz - d))
 
     def slot(self, dy, dx):
         return self.offsets.index((dy % self.ny, dx % self.nx))
-
-    def tile(self, dz):
-        return self.zorder.index(dz % self.nz)
 
 
 def _scratch(p):
     npl, nz, nq = p.plane, p.nz, p.queries
     vm, dma = pltpu.VMEM, pltpu.SemaphoreType.DMA
     groups, most = 2 * npl, max(p.nx, p.ny)
-    nrx = max(groups, 2 * nz)
     chunk = max(p.ch1)
     items = npl * DUO
     return dict(
@@ -113,11 +109,13 @@
         acts=vm((2, ACT_ROWS, DUO), BF16),
         hid=vm((2, DUO, W_A + W_B), BF16),
         unit=vm((2, DUO, DUO), F32),
-        idb=vm((groups, 1, L), I32),
-        lqb=vm((groups, 1, L), F32),
-        idq=vm((nz, 1, L), I32),
-        idk=vm((MAX_GROUPS, L), I32),
+        ids0=vm((1, L), I32),
+        lq0=vm((1, L), F32),
+        inf=vm((groups, 4, L), F32),
+        qinf=vm((nz, 4, L), F32),
         lqk=vm((MAX_GROUPS, L), F32),
+        hik=vm((MAX_GROUPS, L), F32),
+        lok=vm((MAX_GROUPS, L), F32),
         idc=vm((items, L), I32),
         vaug=vm((items, DUO), BF16),
         vt=vm((L, items), BF16),
@@ -126,14 +124,18 @@
         tb=vm((items, nq), F32),
         ls=vm((SUB, nq), F32),
         dg=vm((1, L), F32),
-        stat=vm((nz, 2, nq), F32),
+        lse=vm((2, nq), F32),
+        stat=vm((2, nz, 2, nq // 2), F32),
         fac=vm((2, nq), F32),
         gt=vm((items, nq), BF16),
-        dvp=vm((items, L), F32),
+        dvp=vm((npl * 2, L, L), F32),
         dvs=vm((npl, L, L), F32),
         dvo=vm((npl, L, L), F32),
         dut=vm((nz, L, L), F32),
-        rx=vm((nrx, L, L), F32),
+        rx=vm((2 * nz, L, L), F32),
+        xya=vm((2, most, most, L // 2, L), F32),
+        xyb=vm((2, most, L // 2, L), F32),
+        rv=vm((2, most, 2, L // 2, L), F32),
         de=vm((DUO, L), F32),
         g=vm((GRAD_ROWS, L), F32),
         gc=vm((nz * (p.cz + SUB), L), F32),
@@ -147,9 +149,9 @@
         rc2=vm((p.nx, p.cx + SUB, L), F32),
         rc3=vm((p.ny, p.cx + SUB, L), F32),
         lossb=vm((2, SUB, L), F32),
-        ld=dma((3 + 2 * 4,)),
-        sm_s=dma((3,)),
-        sm_r=dma((3,)),
+        ld=dma((2 + 2 * 4,)),
+        sm_s=dma((2,)),
+        sm_r=dma((2,)),
         v_s=dma((npl,)),
         v_r=dma((npl,)),
         fw_s=dma((npl,)),
@@ -158,13 +160,16 @@
         u_r=dma((nz,)),
         ac_s=dma((3,)),
         ac_r=dma((3,)),
-        st_s=dma((nz,)),
-        st_r=dma((nz,)),
+        st_s=dma((2, nz)),
+        st_r=dma((2, nz)),
         dv_s=dma((npl,)),
         dv_r=dma((npl,)),
-        do_s=dma((npl,)),
+        xy_s=dma((2, most, most)),
+        xy_r=dma((2, most, most)),
+        rv_s=dma((2, most)),
+        rv_r=dma((2, most, 2)),
         du_s=dma((nz,)),
-        rx_r=dma((nrx,)),
+        rx_r=dma((2 * nz,)),
         p1_s=dma((4, most)),
         p1_r=dma((4, most)),
         p2_s=dma((4, most)),
@@ -230,10 +235,8 @@
     other = pl.ds(pl.multiple_of((1 - c) * L, L), L)
 
     mark("start")
-    xs, idb, lqb, idq, ld = s["xs"], s["idb"], s["lqb"], s["idq"], s["ld"]
-    own = p.own
-    small = [(ids, idb.at[c]), (lq, lqb.at[c]), (ids, idq.at[own])]
-    small = [pltpu.make_async_copy(a, b, ld.at[i]) for i, (a, b) in enumerate(small)]
+    xs, inf, qinf, ld = s["xs"], s["inf"], s["qinf"], s["ld"]
+    small = [pltpu.make_async_copy(a, s[b], ld.at[i]) for i, (a, b) in enumerate(((ids, "ids0"), (lq, "lq0")))]
     loads = {}
     n_ld = len(small)
     for t, given in ((ITEM, (ix, iw1, iw2, iw3)), (USER, (ux, uw1, uw2, uw3))):
@@ -276,10 +279,25 @@
 
     mark("towers")
     vaug, uall = s["vaug"], s["uall"]
+
+    def tile_of(zz):
+        return lax.div(zz, 2) + lax.rem(zz, 2) * half
+
+    def z_of(r):
+        return 2 * (r % half) + r // half
+
+    mine = tile_of(z)
     vaug[lane, :L] = tower(ITEM)
-    uall[_lanes(own), :] = tower(USER)
+    uall[pl.ds(pl.multiple_of(mine * L, L), L), :] = tower(USER)
     for cp in small:
         cp.wait()
+    word = 1 << 16
+    id_own, lq_own = s["ids0"][...], s["lq0"][...]
+    told = jnp.concatenate(
+        [lq_own, (id_own // word).astype(F32), (id_own % word).astype(F32), jnp.zeros((1, L), F32)], axis=0
+    )
+    inf[c] = told
+    qinf[mine] = told
     mark("barrier_wait")
     pl.semaphore_wait(barrier, len(others))
 
@@ -287,58 +305,66 @@
     sm_s, sm_r = s["sm_s"], s["sm_r"]
 
     def send_small(k, to):
-        rcopy(idb.at[c], idb.at[2 * k + c], sm_s.at[0], sm_r.at[0], to).start()
-        rcopy(lqb.at[c], lqb.at[2 * k + c], sm_s.at[1], sm_r.at[1], to).start()
-
-    send_small(0, sibling)
+        rcopy(inf.at[c], inf.at[2 * k + c], sm_s.at[0], sm_r.at[0], to).start()
+
     for dy, dx in p.offsets[1:]:
         for core in PAIR:
             send_small(p.slot(-dy, -dx), dev(0, dy, dx, core))
+    send_small(0, sibling)
     n_small = 2 * npl - 1
     for dz in _peers(nz):
-        rcopy(idq.at[own], idq.at[p.tile(-dz)], sm_s.at[2], sm_r.at[2], dev(dz, 0, 0, c)).start()
+        rcopy(qinf.at[mine], qinf.at[mine], sm_s.at[1], sm_r.at[1], dev(dz, 0, 0, c)).start()
+    small_waits = ((inf, n_small), (qinf, nz - 1))
 
     def vpart(k, core):
         return vaug.at[pl.ds(pl.multiple_of(k * DUO + core * L, L), L), pl.ds(0, L)]
 
     def upart(j):
-        return uall.at[_lanes(j)]
+        return uall.at[pl.ds(pl.multiple_of(j * L, L), L)]
 
     send(vpart(0, c), vpart(0, c), s["fw_s"].at[0], s["fw_r"].at[0], sibling)
-    for i in range(1, max(npl, nz)):
-        if i < nz:
-            dz = p.zorder[-1 - i]
-            send(upart(own), upart(p.tile(-dz)), s["u_s"].at[dz], s["u_r"].at[p.tile(-dz)], dev(dz, 0, 0, c))
-        if i < npl:
-            dy, dx = p.offsets[i]
+    z_near = sorted(_peers(nz), key=lambda d: min(d, nz - d))
+    for i in range(max(npl, nz) - 1):
+        if i < nz - 1:
+            dz = z_near[i]
+            send(upart(mine), upart(mine), s["u_s"].at[dz], s["u_r"].at[nz - dz], dev(dz, 0, 0, c))
+        if i + 1 < npl:
+            dy, dx = p.offsets[i + 1]
             k = p.slot(-dy, -dx)
-            send(vpart(0, c), vpart(k, c), s["v_s"].at[i], s["v_r"].at[k], dev(0, dy, dx, c))
+            send(vpart(0, c), vpart(k, c), s["v_s"].at[i + 1], s["v_r"].at[k], dev(0, dy, dx, c))
     for i, part in enumerate(((acts, slice(None), lane), (hid, lane, slice(None)), (unit, lane, slice(None)))):
         ref, rows, cols = part
         send(ref.at[1, rows, cols], ref.at[0, rows, cols], s["ac_s"].at[i], s["ac_r"].at[i], sibling)
 
     mark("small_wait")
-    idk, lqk, idc, ut = s["idk"], s["lqk"], s["idc"], s["ut"]
-    idk[...] = jnp.full(idk.shape, -1, I32)
+    lqk, hik, lok, idc, ut = s["lqk"], s["hik"], s["lok"], s["idc"], s["ut"]
     lqk[...] = jnp.full(lqk.shape, -LOW, F32)
+    hik[...] = jnp.full(hik.shape, -1.0, F32)
+    lok[...] = jnp.full(lok.shape, -1.0, F32)
     ut[L:, :] = jnp.where(_iota((L, nq), 0) < 3 * MAX_GROUPS, -1.0, 0.0).astype(BF16)
-    for i, (ref, n) in enumerate(((idb, n_small), (lqb, n_small), (idq, nz - 1))):
+    for i, (ref, n) in enumerate(small_waits):
         if n:
             pltpu.make_async_copy(ref.at[pl.ds(0, n)], ref.at[pl.ds(0, n)], sm_r.at[i]).wait()
     mark("turn")
+
+    def ident(hi, lo):
+        return hi.astype(I32) * word + lo.astype(I32)
+
     for g in range(2 * npl):
-        row = idb[g]
-        idk[g : g + 1, :] = row
-        lqk[g : g + 1, :] = lqb[g] * TEMP
-        idc[_lanes(g), :] = jnp.broadcast_to(row, (L, L)).T
+        hi, lo = inf[g, 1:2, :], inf[g, 2:3, :]
+        lqk[g : g + 1, :] = inf[g, :1, :] * TEMP
+        hik[g : g + 1, :] = hi
+        lok[g : g + 1, :] = lo
+        idc[_lanes(g), :] = jnp.broadcast_to(ident(hi, lo), (L, L)).T
+    idq = [ident(qinf[r, 1:2, :], qinf[r, 2:3, :]) for r in range(nz)]
 
     def parts(q):
         hi = q.astype(BF16).astype(F32)
         mid = (q - hi).astype(BF16).astype(F32)
         return hi, mid, (q - hi - mid).astype(BF16).astype(F32)
 
-    q_all, id_all = lqk[...], idk[...]
-    split = parts(jnp.where(id_all < 0, 0.0, q_all))
+    q_all, id_hi, id_lo = lqk[...], hik[...], lok[...]
+    split = parts(jnp.where(id_hi < 0.0, 0.0, q_all))
     turned = jnp.concatenate([*split, jnp.zeros((MAX_GROUPS, L), F32)], axis=0).T.astype(BF16)
     col = _iota((L, L), 1)
     ones = jnp.where(col < 3 * MAX_GROUPS + 3, 1.0, 0.0)
@@ -351,35 +377,35 @@
 
     top1 = most(-q_all)
     at_top = -q_all == top1
-    id_hi, id_lo = (id_all // (1 << 16)).astype(F32), (id_all % (1 << 16)).astype(F32)
     top_hi = most(jnp.where(at_top, id_hi, -1.0))
     top_lo = most(jnp.where(jnp.logical_and(at_top, id_hi == top_hi), id_lo, -1.0))
     same_top = jnp.logical_and(id_hi == top_hi, id_lo == top_lo)
     top2 = most(jnp.where(same_top, LOW, -q_all))
     top2 = jnp.where(top2 <= LOW, top1, top2)
-    id_top = top_hi.astype(I32) * (1 << 16) + top_lo.astype(I32)
+    id_top = ident(top_hi, top_lo)
     stat = s["stat"]
     bounds = []
-    for j in range(nz):
-        rest = top2
-        if j == own:
-            rest = jnp.maximum(top2, -lqb[c] * TEMP)
-        bounds.append(jnp.where(idq[j] == id_top, rest, jnp.broadcast_to(top1, (1, L))))
+    for r in range(nz):
+        rest = jnp.maximum(top2, jnp.where(z == z_of(r), -lq_own * TEMP, LOW))
+        bounds.append(jnp.where(idq[r] == id_top, rest, jnp.broadcast_to(top1, (1, L))))
     bound = jnp.concatenate(bounds, axis=1)
-    stat[0, :1, :] = bound
+    ends = (range(half), range(half, nz))
+    for h in PAIR:
+        stat[h, 0, :1, :] = jnp.concatenate([bounds[r] for r in ends[h]], axis=1)
     at = L + 3 * MAX_GROUPS
     ut[at : at + 16, :] = jnp.concatenate([-a for a in parts(bound)] + [jnp.zeros((16 - 3, nq), F32)], axis=0).astype(BF16)
 
+    mark("u_wait")
     tb, ls, vt, dg = s["tb"], s["ls"], s["vt"], s["dg"]
-    ls[...] = jnp.zeros(ls.shape, F32)
-    diag = _iota((DUO, L), 0) == _iota((DUO, L), 1) + c * L
-    far, close = range(half), range(half, nz)
-
-    def queries(tiles):
-        for j in reversed(tiles):
-            if j != own:
-                arrived(upart(j), s["u_r"].at[j])
-            ut[:L, _lanes(j)] = uall[_lanes(j), :].T
+    dg[...] = jnp.zeros(dg.shape, F32)
+    for dz in z_near:
+        arrived(upart(tile_of(lax.rem(z + dz, nz))), s["u_r"].at[dz])
+    for r in range(nz):
+        ut[:L, _lanes(r)] = uall[_lanes(r), :].T
+    item_row, query_at = _iota((DUO, L), 0), _iota((DUO, L), 1) + c * L
+
+    def is_diag(r):
+        return item_row == query_at + jnp.where(z == z_of(r), 0, DUO)
 
     def pass1(blocks, tiles):
         rows = slice(blocks[0] * DUO, (blocks[-1] + 1) * DUO)
@@ -390,13 +416,17 @@
                 at = slice(k * DUO, (k + 1) * DUO)
                 t = wide[n * DUO : (n + 1) * DUO, _lanes(i)]
                 drop = idc[at, :] == idq[r]
-                if k == 0 and r == own:
-                    drop = jnp.logical_and(drop, jnp.logical_not(diag))
-                    dg[...] = jnp.sum(jnp.where(diag, t, 0.0), axis=0, keepdims=True)
+                if k == 0:
+                    pair = is_diag(r)
+                    drop = jnp.logical_and(drop, jnp.logical_not(pair))
+                    dg[...] += jnp.sum(jnp.where(pair, t, 0.0), axis=0, keepdims=True)
                 e = jnp.where(drop, 0.0, jnp.exp2(t * EXP_SCALE))
                 tb[at, _lanes(r)] = e
                 add = add + jnp.sum(e.reshape(DUO // SUB, SUB, L), axis=0)
-            ls[:, _lanes(r)] += add
+            if blocks[0] == 0:
+                ls[:, _lanes(r)] = add
+            else:
+                ls[:, _lanes(r)] += add
 
     def forward(blocks):
         for k in blocks:
@@ -404,71 +434,55 @@
                 arrived(vpart(k, c), s["v_r"].at[k])
                 send(vpart(k, c), vpart(k, c), s["fw_s"].at[k], s["fw_r"].at[k], sibling)
 
-    def whole(blocks):
+    def send_stats(h):
+        cols = _lanes(h * half, half)
+        stat[h, 0, 1:, :] = jnp.sum(ls[:, cols], axis=0, keepdims=True)
+        for dz in _peers(nz):
+            send(stat.at[h, 0], stat.at[h, nz - dz], s["st_s"].at[h, dz], s["st_r"].at[h, nz - dz], dev(dz, 0, 0, c))
+
+    size = min(GROUP, npl)
+    groups = [range(a, a + size) for a in range(0, npl, size)]
+    mark("pass1a")
+    forward(groups[0])
+    for n, blocks in enumerate(groups):
+        if n + 1 < len(groups):
+            forward(groups[n + 1])
         for k in blocks:
             arrived(vpart(k, 1 - c), s["fw_r"].at[k])
-
-    size = min(GROUP, npl)
-    groups = [range(a, a + size) for a in range(0, npl, size)]
-    early = groups[: len(groups) // 2]
-    late = groups[len(early) :]
-    mark("u_close")
-    queries(close)
-    mark("pass1_close")
-    forward(groups[0])
-    for n, blocks in enumerate(early):
-        forward(groups[n + 1])
-        whole(blocks)
-        pass1(blocks, close)
-    mark("u_far")
-    queries(far)
-    mark("pass1_far")
-    for blocks in early:
-        pass1(blocks, far)
-    mark("pass1_late")
-    for n, blocks in enumerate(late):
-        if n + 1 < len(late):
-            forward(late[n + 1])
-        whole(blocks)
-        pass1(blocks, close)
-        pass1(blocks, far)
-
-    mark("stat_send")
-    stat[0, 1:, :] = jnp.sum(ls[...], axis=0, keepdims=True)
-    for dz in _peers(nz):
-        send(stat.at[0], stat.at[nz - dz], s["st_s"].at[dz], s["st_r"].at[nz - dz], dev(dz, 0, 0, c))
-
+        pass1(blocks, ends[0])
+    send_stats(0)
+    mark("pass1b")
+    for blocks in groups:
+        pass1(blocks, ends[1])
+    send_stats(1)
+    mark("flip")
     for k in range(2 * npl):
         vt[:, _lanes(k)] = vaug[_lanes(k), :L].T
-    mark("stat_wait")
-    for dz in _peers(nz):
-        arrived(stat.at[dz], s["st_r"].at[dz])
-
-    def theirs(row, dz):
-        a = stat[dz, row : row + 1, :]
-        return a if dz == 0 else jnp.concatenate([a[:, _lanes(p.tile(d - dz))] for d in p.zorder], axis=1)
-
-    sums = [theirs(1, dz) for dz in range(nz)]
-    tops = [jnp.where(a > 0.0, theirs(0, dz), LOW) for dz, a in enumerate(sums)]
-    top = functools.reduce(jnp.maximum, tops)
-    total = sum(a * jnp.exp2((b - top) * EXP_SCALE) for a, b in zip(sums, tops, strict=True))
-    mine = _lanes(own)
-    loss_part = (top[:, mine] - bound[:, mine] - dg[...]) * INV_TEMP + jnp.log(total[:, mine])
-    loss_tile = jnp.where(_iota((SUB, L), 0) == 0, loss_part, 0.0)
-    fac = s["fac"]
+
+    fac, lse = s["fac"], s["lse"]
     inv_batch = 1.0 / p.batch
-    fac[:1, :] = jnp.exp2((tops[0] - top) * EXP_SCALE) * (1.0 / total)
-    fac[1:, :] = fac[:1, :] * inv_batch
+
+    def statistics(h):
+        cols = _lanes(h * half, half)
+        for dz in _peers(nz):
+            arrived(stat.at[h, dz], s["st_r"].at[h, dz])
+        sums = [stat[h, dz, 1:, :] for dz in range(nz)]
+        tops = [jnp.where(a > 0.0, stat[h, dz, :1, :], LOW) for dz, a in enumerate(sums)]
+        top = functools.reduce(jnp.maximum, tops)
+        total = sum(a * jnp.exp2((b - top) * EXP_SCALE) for a, b in zip(sums, tops, strict=True))
+        fac[:1, cols] = jnp.exp2((tops[0] - top) * EXP_SCALE) * (1.0 / total)
+        fac[1:, cols] = fac[:1, cols] * inv_batch
+        lse[:1, cols] = top - bound[:, cols]
+        lse[1:, cols] = total
 
     gt, dut, dvp, dvs, dvo, rx = s["gt"], s["dut"], s["dvp"], s["dvs"], s["dvo"], s["rx"]
-    plane = y * nx + x
 
     def grads(blocks, tiles):
         for k in blocks:
             at = slice(k * DUO, (k + 1) * DUO)
             for r in tiles:
-                if k == 0 and r == own:
-                    g = (tb[at, _lanes(r)] * fac[:1, _lanes(r)] - jnp.where(diag, 1.0, 0.0)) * inv_batch
+                if k == 0:
+                    g = (tb[at, _lanes(r)] * fac[:1, _lanes(r)] - jnp.where(is_diag(r), 1.0, 0.0)) * inv_batch
                 else:
                     g = tb[at, _lanes(r)] * fac[1:, _lanes(r)]
                 gt[at, _lanes(r)] = g.astype(BF16)
@@ -481,76 +495,134 @@
             dut[r] = piece if first else dut[r] + piece
 
     def item_part(blocks):
-        rows = slice(min(blocks) * DUO, (max(blocks) + 1) * DUO)
-        dvp[rows, :] = _dot(gt[rows, :], uall[...])
-        for k in blocks:
-            src = dvp.at[pl.ds(pl.multiple_of(k * DUO + (1 - c) * L, L), L)]
-            send(src, dvs.at[k], s["dv_s"].at[k], s["dv_r"].at[k], sibling)
-
-    def send_du(tiles):
-        for j in tiles:
-            dz = p.zorder[j]
-            if dz:
-                send(dut.at[j], rx.at[2 * z + c], s["du_s"].at[dz], s["rx_r"].at[2 * z + c], dev(dz, 0, 0, 0))
+        rows = slice(blocks[0] * DUO, (blocks[-1] + 1) * DUO)
+        part = _dot(ut[:L, :], gt[rows, :], NT)
+        for i in range(2 * len(blocks)):
+            dvp[2 * blocks[0] + i] = part[:, _lanes(i)]
+
+    def give_sibling(blocks):
+        for k in reversed(blocks):
+            send(dvp.at[2 * k + 1 - c], dvs.at[k], s["dv_s"].at[k], s["dv_r"].at[k], sibling)
+
+    guarded = []
+
+    def send_du(h):
+        for i, d in enumerate(p.evens):
+            zz = lax.rem(z + d + lax.rem(h + z, 2), nz)
+            to = ((zz * ny + y) * nx + x) * 2
+            cp = rcopy(
+                dut.at[tile_of(zz)], rx.at[2 * z + c], s["du_s"].at[h * half + i], s["rx_r"].at[2 * z + c], to
+            )
+            pl.when(to != me)(cp.start)
+            guarded.append((to != me, cp))
+
+    top_rows, low_rows = pl.ds(0, L // 2), pl.ds(L // 2, L // 2)
+    xya, xyb, rv = s["xya"], s["xyb"], s["rv"]
 
     def finish(blocks):
-        for k in blocks:
+        for k in reversed(blocks):
             arrived(dvs.at[k], s["dv_r"].at[k])
-            dvo[k] = dvp[pl.ds(pl.multiple_of(k * DUO + c * L, L), L), :] + dvs[k]
-            if k:
-                dy, dx = p.offsets[k]
-                send(dvo.at[k], rx.at[2 * plane + c], s["do_s"].at[k], s["rx_r"].at[2 * plane + c], dev(0, dy, dx, 1))
-
+            dvo[k] = dvp[2 * k + c] + dvs[k]
+            dy, dx = p.offsets[k]
+            for part, rows, d, rest, n, to in (
+                (0, top_rows, dx, dy, nx, (0, dx)),
+                (1, low_rows, dy, dx, ny, (dy, 0)),
+            ):
+                if d:
+                    sem = (part, n - d, rest)
+                    send(dvo.at[k, rows], xya.at[sem], s["xy_s"].at[sem], s["xy_r"].at[sem], dev(0, *to, c))
+
+    def second_step(part, d):
+        n = ny if part else nx
+        k = p.offsets.index((0, d) if part else (d, 0))
+        acc = dvo[k, low_rows if part else top_rows, :]
+        for i in reversed(_peers(n)):
+            arrived(xya.at[part, i, d], s["xy_r"].at[part, i, d])
+            acc = acc + xya[part, i, d]
+        m = nx if part else ny
+        if d:
+            xyb[part, d] = acc
+            to = dev(0, 0, d, 1) if part else dev(0, d, 0, 1)
+            send(xyb.at[part, d], rv.at[part, m - d, c], s["rv_s"].at[part, d], s["rv_r"].at[part, m - d, c], to)
+        else:
+            rv[part, 0, c] = acc
+
+    mark("stat_a")
+    statistics(0)
     mark("pass2a")
+    grads(groups[0], ends[0])
     for n, blocks in enumerate(groups):
-        grads(blocks, far)
-        user_part(blocks, far, n == 0)
-    send_du(far)
+        user_part(blocks, ends[0], n == 0)
+        if n + 1 < len(groups):
+            grads(groups[n + 1], ends[0])
+    send_du(0)
+    mark("stat_b")
+    statistics(1)
     mark("pass2b")
+    grads(groups[0], ends[1])
+    for n, blocks in enumerate(groups):
+        user_part(blocks, ends[1], n == 0)
+        if n + 1 < len(groups):
+            grads(groups[n + 1], ends[1])
+    send_du(1)
+    mark("pass2c")
     order, lo = [], npl
     while lo:
         take = min(GROUP if len(order) > 1 else GROUP // 2, lo)
         order.append(range(lo - take, lo))
         lo -= take
     for n, blocks in enumerate(order):
-        grads(blocks, close)
-        item_part(blocks[::-1])
-        user_part(blocks, close, n == 0)
-        if n:
-            finish(order[n - 1][::-1])
-    mark("rs_send")
-    send_du(close)
-    finish(order[-1][::-1])
+        item_part(blocks)
+        give_sibling(blocks)
+        if n >= LAG:
+            finish(order[n - LAG])
+    mark("rs_first")
+    for blocks in order[-LAG:]:
+        finish(blocks)
+    mark("rs_second")
+    for i in reversed(range(max(nx, ny))):
+        for part in PAIR:
+            d = _near(i)
+            if d < (nx if part else ny):
+                second_step(part, d)
+    own_cols = pl.ds(pl.multiple_of(mine * L, L), L)
+    loss_part = (lse[:1, own_cols] - dg[...]) * INV_TEMP + jnp.log(lse[1:, own_cols])
+    loss_tile = jnp.where(_iota((SUB, L), 0) == 0, loss_part, 0.0)
 
     mark("rs_wait")
     de = s["de"]
 
-    def gather(h, acc, order, turn):
+    def gather(h, acc, order):
         for j in order:
             arrived(rx.at[j], s["rx_r"].at[j])
             acc = rx[j] if acc is None else acc + rx[j]
-        de[_lanes(h), :] = (acc.T if turn else acc) * INV_TEMP
-
-    z_from = [lax.rem(z + d, nz) for d in p.zorder if d]
-    plane_from = [
-        lax.rem(y + ny - dy, ny) * nx + lax.rem(x + nx - dx, nx) for dy, dx in reversed(p.offsets[1:])
-    ]
+        de[_lanes(h), :] = acc.T * INV_TEMP
+
+    z_from = [lax.rem(z + d, nz) for d in reversed(z_near)]
 
     @pl.when(c == USER)
     def _():
-        cp = rcopy(dvo.at[0], rx.at[2 * plane], s["do_s"].at[0], s["rx_r"].at[2 * plane], sibling)
-        cp.start()
-        gather(0, dut[own], [2 * a for a in z_from], True)
-        gather(1, None, [2 * a + 1 for a in [*z_from, z]], True)
-        cp.wait_send()
+        cps = []
+        for part in PAIR:
+            cps.append(rcopy(rv.at[part, 0, 0], rv.at[part, 0, 0], s["rv_s"].at[part, 0], s["rv_r"].at[part, 0, 0], sibling))
+            cps[-1].start()
+        gather(0, dut[mine], [2 * a for a in z_from])
+        gather(1, None, [2 * a + 1 for a in [*z_from, z]])
+        for cp in cps:
+            cp.wait_send()
 
     @pl.when(c == ITEM)
     def _():
-        cp = rcopy(dut.at[own], rx.at[2 * z + 1], s["du_s"].at[0], s["rx_r"].at[2 * z + 1], sibling)
-        cp.start()
-        gather(1, dvo[0], [2 * a + 1 for a in plane_from], False)
-        gather(0, None, [2 * a for a in [*plane_from, plane]], False)
-        cp.wait_send()
+        for h in reversed(PAIR):
+            sums = []
+            for part in PAIR:
+                acc = None
+                for d in [*reversed(_peers(nx if part else ny)), 0]:
+                    if d or h == 0:
+                        arrived(rv.at[part, d, h], s["rv_r"].at[part, d, h])
+                    acc = rv[part, d, h] if acc is None else acc + rv[part, d, h]
+                sums.append(acc)
+            de[_lanes(h), :] = jnp.concatenate(sums, axis=0).T * INV_TEMP
 
     mark("backward")
     arrived(acts.at[0, :, other], s["ac_r"].at[0])
@@ -780,12 +852,14 @@
     arrived(fin.at[1 - c, whole_c], s["sb_r"].at[len(STREAMS), 0])
 
     mark("final_waits")
-    for i, (ref, n) in enumerate(((idb, n_small), (lqb, n_small), (idq, nz - 1))):
+    for i, (ref, n) in enumerate(small_waits):
         if n:
             pltpu.make_async_copy(ref.at[pl.ds(0, n)], ref.at[pl.ds(0, n)], sm_s.at[i]).wait()
 
     for cp in sends:
         cp.wait_send()
+    for sent, cp in guarded:
+        pl.when(sent)(cp.wait_send)
     mark()
 
 

time: 87.7 us -> 86.3 us (0.984)
  Pallas kernels: 86.8 us -> 85.4 us
    pallas_call x1, Pallas kernels: 84.8 us -> 83.4 us  [_step(): pl.pallas_call(functools.partial(_kernel, p, tuple(scratch)), out_shape=(...]
where the time goes in v3:
time: 86.3 us; the launch traced here: 86.2 us
  Pallas kernels  85.4 us (99%)
    pallas_call x1, Pallas kernels, _step(): pl.pallas_call(functools.partial(_kernel, p, tuple(scratch)), out_shape=(...  83.4 us
    pallas_call x1, Pallas kernels, _step(): pl.pallas_call(_layout_kernel, out_shape=[jax.ShapeDtypeStruct(a, F32) fo...  2.03 us

profile of v3, /device:TPU:1, one launch (start us, length us, event | category | flops | bytes accessed | tf_op | source)
XLA Modules:
  0.0 86.2 jit_solution(8049930587080532709)
XLA Ops:
  0.6 83.4 %two_tower_step.1 = (f32[2,2304,128]{2,1,0:T(8,128)S(1)}, f32[8,128]{1,0:T(8,128)S(1)}) custom-call(f32[128,256]{1,0:T(8,128)} %ux.1, f32[128,256]{1,0:T(8,128)} %ix.1, s32[1,128]{1,0:T(1,128)} %bitcast.3, f32[1,128]{1,0:T(1,128)} %bitcast.4, f32[256,384]{1,0:T(8,128)} %uw1.1, f32[384,384]{1,0:T(8,128)} %uw2.1, f32[384,128]{1,0:T(8,128)} %uw3.1, ...), custom_call_target="tpu_custom_call" | custom-call | tf_op jit(solution)/shard_map/two_tower_step/pallas_call | solution.py:889
  84.0 2.0 %layout.1 = (f32[256,384]{1,0:T(8,128)}, f32[384,384]{1,0:T(8,128)}, f32[384,128]{1,0:T(8,128)}, f32[256,384]{1,0:T(8,128)}, f32[384,384]{1,0:T(8,128)}, /*index=5*/f32[384,128]{1,0:T(8,128)}, f32[1,1]{1,0:T(1,128)}) custom-call(f32[2,2304,128]{2,1,0:T(8,128)S(1)} %get-tuple-element.16.fin, f32[8,128]{1,0:T(8,128)S(1)} %get-tuple-element.17.loss_in), custom_call_target="tpu_custom_call" | custom-call | tf_op jit(solution)/shard_map/layout/pallas_call | solution.py:899
